TPU v7x, 256 devices: a whole 4x4x8 slice. The times are simulated.
256 devices in a mesh: prow: 16 (over y, x_lo, core), pcol: 16 (over x_hi, z).
Axes of the slice: x: 4 (x_hi: 2, x_lo: 2; x = x_hi * 2 + x_lo), y: 4, z: 8, core: 2. Of those that a mesh axis runs over, the one named last changes fastest.
Arguments:
- ancestor_inverse: float32 [16, 16, 512, 512], P('prow', 'pcol'), may hold values from -0.0625 to 0.0625
- factor_panel: float32 [512, 16, 3, 512], P('pcol', 'prow'), may hold values from -0.75 to 0.75
- pivot_inverse: float32 [3, 512, 512], P(None, 'prow', 'pcol'), may hold values from -6 to 6
- structure: int32 [16, 3], replicated, may hold values from 0 to 1, as said below
Outputs:
- inverse_panel: float32 [512, 16, 3, 512], P('pcol', 'prow')
- diagonal_block: float32 [3, 512, 512], P(None, 'prow', 'pcol')
Inputs may be any that keep to these rules, and one draw needn't show every extreme that they name: structure[J, K] is 1 where ancestor J lies in supernode K's structure and 0 elsewhere; the last ancestor, 15, lies in every supernode's structure.
All inputs are finite; a program needn't handle non-finite values.
Results may differ from a plain program's by a relative error of at most 0.00007.
Values sent between devices are 32-bit elements; how exact they have to be, the bound alone decides.
A program may use at most 64 MiB of HBM per device.

v0:
```python
import jax
import jax.numpy as jnp
from jax import lax
from jax.sharding import Mesh
from jax.sharding import PartitionSpec as P

PCOL = ("pcol_0", "pcol_1")


def in_order(parts, dim):
    parts = jnp.moveaxis(parts, 0, dim)
    shape = parts.shape
    return parts.reshape(*shape[:dim], shape[dim] * shape[dim + 1], *shape[dim + 2 :])


def all_blocks(value, axes, turns):
    parts = value
    for k in turns:
        parts = lax.all_gather(parts, axes[k])
    done = turns[::-1]
    back = [done.index(k) for k in range(len(axes))]
    parts = parts.transpose(*back, *range(len(axes), parts.ndim))
    return parts.reshape(-1, *value.shape)


def gather_axes(value, axes, turns, dim):
    return in_order(all_blocks(value, axes, turns), dim)


def padded_to(lines, count):
    spare = -len(lines) % count
    return jnp.pad(lines, [(0, spare)] + [(0, 0)] * (lines.ndim - 1))


def from_root(value, axis, root):
    lines = jnp.where(lax.axis_index(axis) == root, value, jnp.zeros_like(value)).reshape(
        -1, *value.shape[1:][-1:]
    )
    padded = padded_to(lines, lax.axis_size(axis))
    own = lax.psum_scatter(padded, axis, scatter_dimension=0, tiled=True)
    return lax.all_gather(own, axis, axis=0, tiled=True)[: len(lines)].reshape(value.shape)


def sum_in_order(parts, axes, turns):
    shape = [lax.axis_size(a) for a in axes]
    parts = parts.reshape(*shape, *parts.shape[1:])
    parts = parts.transpose(*turns, *range(len(axes), parts.ndim))
    parts = parts.reshape(-1, *parts.shape[len(axes) :])
    for k in turns:
        parts = lax.psum_scatter(parts, axes[k], scatter_dimension=0, tiled=True)
    return parts[0]


def split_up(value, dim, count):
    before, after = (value.shape[:dim], value.shape[dim + 1 :])
    return jnp.moveaxis(value.reshape(*before, count, -1, *after), dim, 0)


def scatter_axes(value, axes, turns, dim):
    count = lax.axis_size(axes)
    return sum_in_order(split_up(value, dim, count), axes, turns)


def summed_on_arrival(value, axis, dim):
    count = lax.axis_size(axis)
    parts = lax.all_to_all(split_up(value, dim, count), axis, 0, 0, tiled=True)
    return jnp.sum(parts, axis=0)


def keep_same(running):
    return running


def body(ancestor_inverse, factor_panel, pivot_inverse, structure):
    row_count = ancestor_inverse.shape[0]
    col_count = ancestor_inverse.shape[1]
    width = ancestor_inverse.shape[3]
    ratio = lax.axis_size("prow") // lax.axis_size(PCOL)
    grid_row = lax.axis_index("prow")
    grid_col = lax.axis_index(PCOL)
    struct_float = structure.astype(jnp.float32)
    own_mask = lax.dynamic_slice_in_dim(struct_float, grid_row * row_count, row_count, 0)
    col_mask = lax.dynamic_slice_in_dim(structure, grid_col * col_count, col_count, 0)
    row_panel = gather_axes(factor_panel, PCOL, (0, 1), 0)
    masked_rows = row_panel * own_mask[None, :, :, None]
    member = 0
    pieces = from_root(row_panel, "prow", grid_col * ratio + member)
    count_here = pieces.shape[2]
    running = jnp.zeros((width, row_count, count_here, width), jnp.float32)
    member = 0
    for super_index in range(count_here):

        def add_block(
            total,
            inverse_block=ancestor_inverse[0, member],
            factor_block=pieces[:, member, super_index, :],
            position=super_index,
            row_at=0,
        ):
            update = jnp.dot(
                inverse_block,
                factor_block,
                precision=lax.Precision.HIGHEST,
                preferred_element_type=jnp.float32,
            )
            return total.at[:, row_at, position, :].add(update)

        needed = jnp.logical_and(col_mask[member, super_index] > 0, own_mask[0, super_index] > 0)
        running = lax.cond(needed, add_block, keep_same, running)
    share = scatter_axes(running, PCOL, (1, 0), 0)
    diagonal_term = -jnp.einsum(
        "riKa,riKb->Kab",
        masked_rows,
        running,
        precision=lax.Precision.HIGHEST,
        preferred_element_type=jnp.float32,
    )
    share, diagonal_term = (share, diagonal_term)
    inverse_panel = -own_mask[None, :, :, None] * share
    by_rows = summed_on_arrival(diagonal_term, "prow", 1)
    by_both = summed_on_arrival(by_rows, PCOL, 2)
    return (inverse_panel, pivot_inverse - by_both)


def solution(mesh):
    torus = Mesh(mesh.devices.reshape(mesh.shape["prow"], 2, 8), ("prow", "pcol_0", "pcol_1"))
    return jax.shard_map(
        body,
        mesh=torus,
        in_specs=(
            P("prow", PCOL, None, None),
            P(PCOL, "prow", None, None),
            P(None, "prow", PCOL),
            P(),
        ),
        out_specs=(P(PCOL, "prow", None, None), P(None, "prow", PCOL)),
        check_vma=False,
    )
```

profile of v0, /device:TPU:7, one launch (start us, length us, event | category | flops | bytes accessed | tf_op | source)
XLA Modules:
  0.0 299.0 jit_solution(8792539804364169806)
XLA Ops:
  7.2 0.9 copy.42
  8.2 8.1 %all-gather = f32[64,1,3,512]{3,0,2,1:T(8,128)} all-gather(f32[32,1,3,512]{3,0,2,1:T(8,128)S(1)} %copy.42), channel_id=2, replica_groups=mesh['prow'=16,'pcol_0'=2,'pcol_1'=8] {'pcol_0'}, dimensions={0}, use_global_device_ids=true | all-gather | bytes 589824 | tf_op jit(solution)/shard_map/all_gather | solution.py:19
  16.3 48.3 %all-gather.7.cloned.1.call-done = f32[16,32,1,3,512]{4,1,0,3,2:T(8,128)} async-done(((f32[2,32,1,3,512]{4,1,0,3,2:T(8,128)}), f32[16,32,1,3,512]{4,1,0,3,2:T(8,128)}) %all-gather.7.cloned.1.call-update) | async-done | bytes 3145744 | tf_op jit(solution)/shard_map/all_gather | solution.py:19
  64.6 2.2 copy.43
  66.8 1.7 copy-done
  68.5 0.6 broadcast_select_fusion
  69.1 4.1 %copy.44 = f32[2,8,32,1,3,512]{5,4,2,1,0,3:T(4,128)} copy(f32[2,8,32,1,3,512]{5,2,4,3,0,1:T(8,128)S(1)} %broadcast_select_fusion) | data formatting | bytes 6291456 | tf_op jit(solution)/shard_map/jit(_where)/select_n | solution.py:36
  73.2 6.0 %select_n.24 = f32[1536,512]{1,0:T(8,128)} reshape(f32[2,8,32,1,3,512]{5,4,2,1,0,3:T(4,128)} %copy.44) | data formatting | bytes 6291456 | tf_op jit(solution)/shard_map/jit(_where)/select_n | solution.py:36
  79.2 62.8 %reduce-scatter.4.cloned.1.call-done = f32[96,512]{1,0:T(8,128)} async-done(((f32[1536,512]{1,0:T(8,128)}), f32[96,512]{1,0:T(8,128)}) %reduce-scatter.4.cloned.1.call-update) | async-done | bytes 196624 | tf_op jit(solution)/shard_map/reduce_scatter | solution.py:40
  142.2 0.6 fusion.20
  143.7 0.6 fusion.19
  147.4 39.6 %all-gather.5.cloned.1.call-done = f32[1536,512]{1,0:T(8,128)} async-done(((f32[96,512]{1,0:T(8,128)}), f32[1536,512]{1,0:T(8,128)}) %all-gather.5.cloned.1.call-update) | async-done | bytes 3145744 | tf_op jit(solution)/shard_map/all_gather | solution.py:41
  187.1 5.8 %reshape.202 = f32[512,1,3,512]{3,2,0,1:T(4,128)} reshape(f32[1536,512]{1,0:T(8,128)} %all-gather.5.cloned.1.call-done) | data formatting | bytes 6291456 | tf_op jit(solution)/shard_map/reshape | solution.py:41
  192.9 0.4 conditional.3
  192.9 0.4 broadcast.95
  193.5 2.0 copy.48
  195.5 2.2 copy.49
  197.8 5.6 %fusion.12 = f32[3,512,512]{2,1,0:T(8,128)S(1)} fusion(f32[512,1,3,512]{3,0,2,1:T(8,128)S(1)} %get-tuple-element.133, f32[512,3,512]{2,0,1:T(8,128)S(1)} %bitcast.66, f32[3]{0:T(128)S(1)} %get-tuple-element.123), kind=kOutput, calls=%fused_computation.19 | convolution fusion | flops 4833411072 | bytes 9437196 | tf_op jit(solution)/shard_map/riKa,riKb->Kab/dot_general | solution.py:111
  203.4 2.0 copy.71
  205.4 27.9 %all-to-all-start = ((f32[16,3,32,512]{3,2,1,0:T(8,128)}), f32[16,3,32,512]{3,2,1,0:T(8,128)S(1)}, u32[]{:S(2)}, u32[]{:S(2)}) async-start(f32[16,3,32,512]{3,2,1,0:T(8,128)} %bitcast.65), calls=%async_computation.3 | async-start | bytes 6291456 | tf_op jit(solution)/shard_map/all_to_all | solution.py:66
  233.3 28.0 %reduce-scatter.6.cloned.1.call-done = f32[2,32,1,3,512]{4,1,3,2,0:T(8,128)} async-done(((f32[16,32,1,3,512]{4,1,3,2,0:T(8,128)}), f32[2,32,1,3,512]{4,1,3,2,0:T(8,128)}) %reduce-scatter.6.cloned.1.call-update) | async-done | bytes 393232 | tf_op jit(solution)/shard_map/reduce_scatter | solution.py:50
  261.3 9.8 %all-to-all-done = f32[16,3,32,512]{3,2,1,0:T(8,128)S(1)} async-done(((f32[16,3,32,512]{3,2,1,0:T(8,128)}), f32[16,3,32,512]{3,2,1,0:T(8,128)S(1)}, u32[]{:S(2)}, u32[]{:S(2)}) %all-to-all-start) | async-done | bytes 3145760 | tf_op jit(solution)/shard_map/all_to_all | solution.py:66
  271.1 0.3 reduce_sum.18
  271.6 0.3 copy.52
  271.9 1.0 reshape.213
  272.9 7.9 %all-to-all-start.1 = ((f32[16,1,3072]{2,1,0:T(1,128)}), f32[16,1,3072]{2,1,0:T(1,128)S(1)}, u32[]{:S(2)}, u32[]{:S(2)}) async-start(f32[16,1,3072]{2,1,0:T(1,128)} %reshape.213), calls=%async_computation.4 | async-start | bytes 393216 | tf_op jit(solution)/shard_map/all_to_all | solution.py:66
  280.8 7.2 %all-to-all-done.1 = f32[16,1,3072]{2,1,0:T(1,128)S(1)} async-done(((f32[16,1,3072]{2,1,0:T(1,128)}), f32[16,1,3072]{2,1,0:T(1,128)S(1)}, u32[]{:S(2)}, u32[]{:S(2)}) %all-to-all-start.1) | async-done | bytes 196640 | tf_op jit(solution)/shard_map/all_to_all | solution.py:66
  288.0 0.5 broadcast.108
  288.5 1.1 reduce.13
  290.0 0.6 sub.3
  290.6 1.0 bitcast_multiply_fusion
  291.6 0.9 copy.53
  (25 shorter events, 1.3 us)
Async XLA Ops:
  7.2 57.4 %all-gather.7.cloned.1.call-start = ((), (), s32[]{:S(2)}) async-start(), calls=%async_computation.9 | async-start | bytes 3538944 | tf_op jit(solution)/shard_map/all_gather | solution.py:19
  16.2 125.8 %reduce-scatter.4.cloned.1.call-start = ((), (), s32[]{:S(2)}) async-start(), calls=%async_computation.5 | async-start | bytes 3342336 | tf_op jit(solution)/shard_map/reduce_scatter | solution.py:40
  66.8 1.7 copy-start
  79.2 62.9 %copy-start.2 = (s32[16,3]{0,1:T(4,128)S(1)}, s32[16,3]{0,1:T(4,128)}, u32[]{:S(2)}) copy-start(s32[16,3]{0,1:T(4,128)} %param.19) | copy-start | bytes 580
  79.2 107.9 %all-gather.5.cloned.1.call-start = ((), (), s32[]{:S(2)}) async-start(), calls=%async_computation.6 | async-start | bytes 3342336 | tf_op jit(solution)/shard_map/all_gather | solution.py:41
  142.0 119.2 %reduce-scatter.6.cloned.1.call-start = ((), (), s32[]{:S(2)}) async-start(), calls=%async_computation.7 | async-start | bytes 3538944 | tf_op jit(solution)/shard_map/reduce_scatter | solution.py:50
  205.4 65.7 %all-to-all-start = ((f32[16,3,32,512]{3,2,1,0:T(8,128)}), f32[16,3,32,512]{3,2,1,0:T(8,128)S(1)}, u32[]{:S(2)}, u32[]{:S(2)}) async-start(f32[16,3,32,512]{3,2,1,0:T(8,128)} %bitcast.65), calls=%async_computation.3 | async-start | bytes 6291456 | tf_op jit(solution)/shard_map/all_to_all | solution.py:66
  233.3 57.3 %reduce-scatter.8.cloned.1.call-start = ((), (), s32[]{:S(2)}) async-start(), calls=%async_computation.8 | async-start | bytes 589824 | tf_op jit(solution)/shard_map/reduce_scatter | solution.py:50
  271.4 18.6 %copy-start.1 = (f32[3,32,32]{2,1,0:T(8,128)S(1)}, f32[3,32,32]{2,1,0:T(8,128)}, u32[]{:S(2)}) copy-start(f32[3,32,32]{2,1,0:T(8,128)} %param.18) | copy-start | bytes 36868
  272.9 15.1 %all-to-all-start.1 = ((f32[16,1,3072]{2,1,0:T(1,128)}), f32[16,1,3072]{2,1,0:T(1,128)S(1)}, u32[]{:S(2)}, u32[]{:S(2)}) async-start(f32[16,1,3072]{2,1,0:T(1,128)} %reshape.213), calls=%async_computation.4 | async-start | bytes 393216 | tf_op jit(solution)/shard_map/all_to_all | solution.py:66
Sparse Core Ops, SparseCore 0:
  16.4 48.1 all-gather.6
  79.3 62.6 reduce-scatter.3
  143.9 43.1 all-gather.4
  195.7 65.5 reduce-scatter.5
  263.6 20.8 reduce-scatter.7
where the time goes:
time: 304 us; the launch traced here: 299 us
  waiting for transfers between devices  196 us (64%)
  starting transfers between devices  36 us (12%)
  local copies, waits for them, and re-layouts  32 us (11%)
  between operations  17.8 us (6%)
  blocking collectives  8.06 us (3%)
  matrix products  5.56 us (2%)
  other arithmetic  3.72 us (1%)
    reduce_scatter x1, waiting for transfers between devices, from_root(): own = lax.psum_scatter(padded, axis, scatter_dimension=0, tiled=True)  62.8 us
    all_gather x1, waiting for transfers between devices, all_blocks(): parts = lax.all_gather(parts, axes[k])  48.3 us
    all_gather x1, waiting for transfers between devices, from_root(): lax.all_gather(own, axis, axis=0, tiled=True)[:len(lines)]  39.6 us
    all_to_all x2, starting transfers between devices, summed_on_arrival(): parts = lax.all_to_all(split_up(value, dim, count), axis, 0, 0, tiled=True)  35.8 us
    reduce_scatter x2, waiting for transfers between devices, sum_in_order(): parts = lax.psum_scatter(parts, axes[k], scatter_dimension=0, tiled=True)  28 us
    all_to_all x2, waiting for transfers between devices, summed_on_arrival(): parts = lax.all_to_all(split_up(value, dim, count), axis, 0, 0, tiled=True)  17 us
    select_n x2, local copies, waits for them, and re-layouts, from_root(): jnp.where(lax.axis_index(axis) == root, value, jnp.zeros_like(value))  10.1 us
    all_gather x1, blocking collectives, all_blocks(): parts = lax.all_gather(parts, axes[k])  8.06 us
  transfers between devices with their start and end apart: 7, of which 6 were waited for; matrix products, arithmetic and copies ran while one was open for 5% of the time, Pallas kernels for 0%

commit v1 on v0

v1 whole, which is shorter than its diff:
```python
import jax
import jax.numpy as jnp
from jax import lax
from jax.experimental import pallas as pl
from jax.experimental.pallas import tpu as pltpu
from jax.sharding import PartitionSpec as P

F32 = jnp.float32
BF16 = jnp.bfloat16
MESH = pl.DeviceIdType.MESH
ROWS = 32
NSUP = 3
WIDTH = 512
GRID = 16


def split(x):
    high = x.astype(BF16)
    return high, (x - high.astype(F32)).astype(BF16)


def dot(a, b):
    return jnp.dot(a, b, preferred_element_type=F32)


def landing(block, chunk):
    shift = (block - chunk) & 7
    flip = ((block >> 3) ^ (chunk >> 3)) & 1
    turn = jnp.minimum(shift, 8 - shift) & 3
    core = (shift >= 4).astype(jnp.int32)
    return 4 * (((block >> 2) + turn) & 3) + 2 * (((block >> 1) & 1) ^ flip) + core


def chunk_at(row, block):
    turn = ((row >> 2) - (block >> 2)) & 3
    flip = ((row >> 1) & 1) ^ ((block >> 1) & 1)
    back = jnp.where(turn == 0, 4, 8 - turn)
    shift = jnp.where((row & 1) == 1, back, turn)
    return 8 * ((block >> 3) ^ flip) + (((block & 7) - shift) & 7)


def pack(y, put):
    lane = lax.broadcasted_iota(jnp.int32, (8, 128), 1) >> 5
    for g in range(4):
        tiles = [y[8 * u : 8 * u + 8, 128 * g : 128 * g + 128] for u in range(4)]
        for h in range(4):
            out = None
            for u in range(4):
                by = (32 * (u - h)) % 128
                moved = pltpu.roll(tiles[u], by, 1) if by else tiles[u]
                out = moved if out is None else jnp.where(lane == u, moved, out)
            put(4 * g + h, out)


def kernel(
    a_hbm, l_hbm, piv_ref, s_ref,
    y_hbm, d_ref,
    a_in, l_in, a_high, a_low, src, xbuf, pbuf, rbuf, sbuf, xrec, y_out,
    e1s, e1r, e2s, e2r,
    load_sem, ag_send, ag_recv, rs_send, rs_recv, xs_send, xs_recv,
    e1_send, e1_recv, e2_send, e2_recv,
):
    p = lax.axis_index("prow")
    q = lax.axis_index("pcol")
    z = q & 7
    far = q >> 3
    on_diagonal = p == q

    load_l = pltpu.make_async_copy(l_hbm, l_in, load_sem.at[0])
    load_l.start()
    load_a = pltpu.make_async_copy(a_hbm, a_in, load_sem.at[1])
    load_a.start()

    other = p ^ 1
    beside = p ^ 2
    above = (p + 4) & 15
    below = (p - 4) & 15
    z_up = (q & 8) + ((z + 1) & 7)
    z_down = (q & 8) + ((z - 1) & 7)
    across = q ^ 8

    barrier = pltpu.get_barrier_semaphore()
    for device in ((other, q), (beside, q), (above, q), (below, q), (p, z_up), (p, z_down), (p, across)):
        pl.semaphore_signal(barrier, inc=1, device_id=device, device_id_type=MESH)

    def greet(t, carry):
        @pl.when(jnp.logical_or(t != p, p != q))
        def _():
            pl.semaphore_signal(barrier, inc=1, device_id=(t, p), device_id_type=MESH)

        @pl.when(jnp.logical_or(t != q, p != q))
        def _():
            pl.semaphore_signal(barrier, inc=1, device_id=(q, t), device_id_type=MESH)

        return carry

    lax.fori_loop(0, GRID, greet, 0)

    load_l.wait()
    for k in range(NSUP):
        for g in range(4):
            src[k, :, 128 * g : 128 * g + 128] = l_in[pl.ds(4 * k + g, ROWS, stride=12), :]
    load_a.wait()
    a_high[...], a_low[...] = split(a_in[...])
    pl.semaphore_wait(barrier, jnp.where(on_diagonal, 37, 39))

    def remote(source, target, send, recv, device):
        return pltpu.make_async_remote_copy(
            src_ref=source, dst_ref=target, send_sem=send, recv_sem=recv, device_id=device, device_id_type=MESH
        )

    def rows_of(row):
        return pl.ds(pl.multiple_of(ROWS * chunk_at(row, q), ROWS), ROWS)

    kinds = (p, p ^ 2, below, below ^ 2, above, above ^ 2, (p + 8) & 15, ((p + 8) & 15) ^ 2)
    kinds = kinds + tuple(kind ^ 1 for kind in kinds)
    where = [rows_of(kind) for kind in kinds]

    def piece(k, kind):
        return xbuf.at[k, where[kind], :]

    sends = []

    def send_piece(k, kind, slot, as_kind, device):
        copy = remote(piece(k, kind), piece(k, kind), ag_send.at[k, slot], ag_recv.at[k, as_kind], (device, q))
        copy.start()
        sends.append(copy)

    def wait_piece(k, kind):
        remote(piece(k, kind), piece(k, kind), ag_send.at[k, 0], ag_recv.at[k, kind], (other, q)).wait_recv()

    first = landing(p, q)
    first_rows = pl.ds(pl.multiple_of(ROWS * q, ROWS), ROWS)
    stays = jnp.logical_and(first == p, on_diagonal)

    def first_copy(k):
        return remote(src.at[k], xbuf.at[k, first_rows, :], ag_send.at[k, 0], ag_recv.at[k, 0], (first, p))

    def st_first(k):
        @pl.when(jnp.logical_not(stays))
        def _():
            first_copy(k).start()

        @pl.when(stays)
        def _():
            xbuf[k, first_rows, :] = src[k]

    mine = jnp.logical_and(landing(q, q) == p, on_diagonal)

    def st_own(k):
        @pl.when(jnp.logical_not(mine))
        def _():
            wait_piece(k, 0)

        send_piece(k, 0, 1, 1, beside)
        send_piece(k, 0, 2, 2, above)
        send_piece(k, 0, 3, 4, below)
        send_piece(k, 0, 8, 8, other)

    def st_beside(k):
        wait_piece(k, 1)
        send_piece(k, 1, 4, 3, above)
        send_piece(k, 1, 5, 5, below)
        send_piece(k, 1, 9, 9, other)

    def st_ring(k):
        wait_piece(k, 2)
        send_piece(k, 2, 6, 6, above)
        send_piece(k, 2, 10, 10, other)
        wait_piece(k, 4)
        send_piece(k, 4, 12, 12, other)
        wait_piece(k, 5)
        send_piece(k, 5, 7, 7, below)
        send_piece(k, 5, 13, 13, other)
        wait_piece(k, 3)
        send_piece(k, 3, 11, 11, other)

    def st_last(k):
        wait_piece(k, 6)
        send_piece(k, 6, 14, 14, other)
        wait_piece(k, 7)
        send_piece(k, 7, 15, 15, other)

    down_steps = (4, 3)
    up_steps = (3, 4)
    steps = [[down_steps[h], up_steps[h]] for h in range(2)]

    def block_rows(h, d):
        return pl.ds(pl.multiple_of(256 * h + ROWS * d, ROWS), ROWS)

    def sent_block(h, way, t):
        left = steps[h][way] - t
        return (z - left) & 7 if way == 0 else (z + left) & 7

    def send_sum(k, h, way, t):
        copy = remote(
            pbuf.at[k, block_rows(h, sent_block(h, way, t)), :],
            rbuf.at[k, h, way, t],
            rs_send.at[k, h, way, t],
            rs_recv.at[k, h, way, t],
            (p, z_down if way == 0 else z_up),
        )
        copy.start()
        sends.append(copy)

    def wait_sum(k, h, way, t):
        remote(
            rbuf.at[k, h, way, t], rbuf.at[k, h, way, t], rs_send.at[k, h, way, t], rs_recv.at[k, h, way, t], (p, z_up)
        ).wait_recv()

    def mask_of(k, index):
        return s_ref[k, index].astype(F32)

    def st_product(k):
        for kind in range(8, 16):
            wait_piece(k, kind)
        mask = mask_of(k, q)
        x_high, x_low = split(xbuf[k] * mask)
        for m in range(4):
            at = slice(128 * m, 128 * m + 128)
            pbuf[k, at, :] = dot(a_high[at, :], x_high) + dot(a_high[at, :], x_low) + dot(a_low[at, :], x_high)
        for h in range(2):
            for way in range(2):
                send_sum(k, h, way, 0)

    def st_sum(k, t):
        for h in range(2):
            for way in range(2):
                last = steps[h][way] - 1
                if t > last:
                    continue
                wait_sum(k, h, way, t)
                if t < last:
                    rows = block_rows(h, sent_block(h, way, t + 1))
                    pbuf[k, rows, :] = pbuf[k, rows, :] + rbuf[k, h, way, t]
                    send_sum(k, h, way, t + 1)
        if t == 3:
            for h in range(2):
                total = pbuf[k, block_rows(h, z), :]
                for way in range(2):
                    total = total + rbuf[k, h, way, steps[h][way] - 1]
                sbuf[k, h] = total
            copy = remote(sbuf.at[k, 1 - far], xrec.at[k], xs_send.at[k], xs_recv.at[k], (p, across))
            copy.start()
            sends.append(copy)

    def exchange(k, source, target, send, recv):
        def copy(t):
            return remote(source.at[k, t], target.at[k, q], send.at[k, t], recv.at[k, q], (t, p))

        def one(i, carry):
            copy((p + i) & 15).start()
            return carry

        @pl.when(jnp.logical_not(on_diagonal))
        def _():
            copy(p).start()

        @pl.when(on_diagonal)
        def _():
            target[k, q] = source[k, p]

        lax.fori_loop(1, GRID, one, 0)

    def arrived(k, target, send, recv):
        def one(j, carry):
            @pl.when(jnp.logical_or(j != q, p != q))
            def _():
                remote(target.at[k, j], target.at[k, j], send.at[k, j], recv.at[k, j], (other, q)).wait_recv()

            return carry

        lax.fori_loop(0, GRID, one, 0)

    def left(k, source, send, recv):
        def one(t, carry):
            @pl.when(jnp.logical_or(t != p, p != q))
            def _():
                remote(source.at[k, t], source.at[k, t], send.at[k, t], recv.at[k, t], (other, q)).wait_send()

            return carry

        lax.fori_loop(0, GRID, one, 0)

    def st_panel(k):
        remote(xrec.at[k], xrec.at[k], xs_send.at[k], xs_recv.at[k], (p, across)).wait_recv()
        y = (sbuf[k, far] + xrec[k]) * (-mask_of(k, p))

        def put(t, tile):
            e1s[k, t] = tile

        pack(y, put)
        exchange(k, e1s, e1r, e1_send, e1_recv)
        for g in range(4):
            y_out[pl.ds(4 * k + g, ROWS, stride=12), :] = y[:, 128 * g : 128 * g + 128]

    def st_diagonal(k):
        arrived(k, e1r, e1_send, e1_recv)
        turned = e1r[k].reshape(128, 128).T
        x = xbuf[k].reshape(GRID, 4, 8, WIDTH)
        total = None
        for u in range(4):
            y_high, y_low = split(turned[32 * u : 32 * u + 32, :])
            x_high, x_low = split(x[:, u].reshape(128, WIDTH))
            term = dot(y_high, x_high) + dot(y_high, x_low) + dot(y_low, x_high)
            total = term if total is None else total + term

        def put(t, tile):
            e2s[k, t] = tile

        pack(total, put)
        exchange(k, e2s, e2r, e2_send, e2_recv)

    def st_result(k):
        arrived(k, e2r, e2_send, e2_recv)
        total = jnp.sum(e2r[k], axis=0)
        parts = [total] + [pltpu.roll(total, 128 - 32 * u, 1) for u in range(1, 4)]
        square = jnp.concatenate(parts + [jnp.zeros((96, 128), F32)], axis=0).T
        d_ref[k] = piv_ref[k] - square[:32, :32]

    events = []
    for k in range(NSUP):
        events.append((-10 + k, k, st_first))
        events.append((0 + 3 * k, k, st_own))
        events.append((2.5 + 3 * k, k, st_beside))
        events.append((5 + 4 * k, k, st_ring))
        events.append((8 + 4 * k, k, st_last))
        events.append((10 + 4 * k, k, st_product))
        for t in range(4):
            events.append((14 + 4.5 * t + 6 * k, k, lambda k, t=t: st_sum(k, t)))
        events.append((32 + 6 * k, k, st_panel))
        events.append((40 + 6 * k, k, st_diagonal))
        events.append((48 + 6 * k, k, st_result))
    for _, k, stage in sorted(events, key=lambda e: e[0]):
        stage(k)

    store = pltpu.make_async_copy(y_out, y_hbm, load_sem.at[0])
    store.start()
    for k in range(NSUP):

        @pl.when(jnp.logical_not(stays))
        def _():
            first_copy(k).wait_send()

        left(k, e1s, e1_send, e1_recv)
        left(k, e2s, e2_send, e2_recv)
    for copy in sends:
        copy.wait_send()
    store.wait()


def body(ancestor_inverse, factor_panel, pivot_inverse, structure):
    vmem = pl.BlockSpec(memory_space=pltpu.VMEM)
    hbm = pl.BlockSpec(memory_space=pl.ANY)
    dma = pltpu.SemaphoreType.DMA
    panel, diagonal = pl.pallas_call(
        kernel,
        out_shape=(
            jax.ShapeDtypeStruct((ROWS * NSUP * 4, 128), F32),
            jax.ShapeDtypeStruct(pivot_inverse.shape, F32),
        ),
        in_specs=[hbm, hbm, vmem, pl.BlockSpec(memory_space=pltpu.SMEM)],
        out_specs=(hbm, vmem),
        scratch_shapes=[
            pltpu.VMEM((WIDTH, WIDTH), F32),
            pltpu.VMEM((ROWS * NSUP * 4, 128), F32),
            pltpu.VMEM((WIDTH, WIDTH), BF16),
            pltpu.VMEM((WIDTH, WIDTH), BF16),
            pltpu.VMEM((NSUP, ROWS, WIDTH), F32),
            pltpu.VMEM((NSUP, WIDTH, WIDTH), F32),
            pltpu.VMEM((NSUP, WIDTH, WIDTH), F32),
            pltpu.VMEM((NSUP, 2, 2, 4, ROWS, WIDTH), F32),
            pltpu.VMEM((NSUP, 2, ROWS, WIDTH), F32),
            pltpu.VMEM((NSUP, ROWS, WIDTH), F32),
            pltpu.VMEM((ROWS * NSUP * 4, 128), F32),
            pltpu.VMEM((NSUP, GRID, 8, 128), F32),
            pltpu.VMEM((NSUP, GRID, 8, 128), F32),
            pltpu.VMEM((NSUP, GRID, 8, 128), F32),
            pltpu.VMEM((NSUP, GRID, 8, 128), F32),
            dma((2,)),
            dma((NSUP, 16)),
            dma((NSUP, 16)),
            dma((NSUP, 2, 2, 4)),
            dma((NSUP, 2, 2, 4)),
            dma((NSUP,)),
            dma((NSUP,)),
            dma((NSUP, GRID)),
            dma((NSUP, GRID)),
            dma((NSUP, GRID)),
            dma((NSUP, GRID)),
        ],
        compiler_params=pltpu.CompilerParams(
            collective_id=0, has_side_effects=True, vmem_limit_bytes=48 * 1024 * 1024
        ),
        name="level",
    )(
        ancestor_inverse.reshape(WIDTH, WIDTH),
        factor_panel.reshape(ROWS * NSUP * 4, 128),
        pivot_inverse,
        structure.T,
    )
    return panel.reshape(ROWS, 1, NSUP, WIDTH), diagonal


def solution(mesh):
    return jax.shard_map(
        body,
        mesh=mesh,
        in_specs=(
            P("prow", "pcol", None, None),
            P("pcol", "prow", None, None),
            P(None, "prow", "pcol"),
            P(),
        ),
        out_specs=(P("pcol", "prow", None, None), P(None, "prow", "pcol")),
        check_vma=False,
    )
```

time: 304 us -> 119 us (0.39); the launches traced: 299 us -> 119 us
  waiting for transfers between devices: 196 us -> 0 us
  Pallas kernels: 0 us -> 113 us
  starting transfers between devices: 36 us -> 0 us
  local copies, waits for them, and re-layouts: 32 us -> 4.92 us
  between operations: 17.8 us -> 0.65 us
  blocking collectives: 8.06 us -> 0 us
  matrix products: 5.56 us -> 0 us
  other arithmetic: 3.72 us -> 0 us
    pallas_call x0 -> x1, Pallas kernels: none -> 113 us  [body(): pl.pallas_call(kernel, out_shape=(jax.ShapeDtypeStruct((ROWS * NSUP * 4,...]
    reduce_scatter x3 -> x0, waiting for transfers between devices: 90.7 us -> none  [the longest x1 62.8 us: from_root(): own = lax.psum_scatter(padded, axis, scatter_dimension=0, tiled=True)]
    all_gather x2 -> x0, waiting for transfers between devices: 87.9 us -> none  [the longest x1 48.3 us: all_blocks(): parts = lax.all_gather(parts, axes[k])]
    all_to_all x2 -> x0, starting transfers between devices: 35.8 us -> none  [summed_on_arrival(): parts = lax.all_to_all(split_up(value, dim, count), axis, 0, 0, tiled=True)]
    all_to_all x2 -> x0, waiting for transfers between devices: 17 us -> none  [summed_on_arrival(): parts = lax.all_to_all(split_up(value, dim, count), axis, 0, 0, tiled=True)]
    select_n x2 -> x0, local copies, waits for them, and re-layouts: 10.1 us -> none  [from_root(): jnp.where(lax.axis_index(axis) == root, value, jnp.zeros_like(value))]
    reshape x3 -> x0, local copies, waits for them, and re-layouts: 8.07 us -> none  [the longest x1 5.8 us: from_root(): lax.all_gather(own, axis, axis=0, tiled=True)[:len(lines)]]
    all_gather x1 -> x0, blocking collectives: 8.06 us -> none  [all_blocks(): parts = lax.all_gather(parts, axes[k])]
  transfers between devices with their start and end apart: 7 -> 0, of which waited for: 6 -> 0; matrix products, arithmetic and copies ran while one was open for 5% -> 0% of each run, Pallas kernels for 0% -> 0%
where the time goes in v1:
time: 119 us
  Pallas kernels  113 us (95%)
  local copies, waits for them, and re-layouts  4.92 us (4%)
    pallas_call x1, Pallas kernels, body(): pl.pallas_call(kernel, out_shape=(jax.ShapeDtypeStruct((ROWS * NSUP * 4,...  113 us
    unnamed x10, local copies, waits for them, and re-layouts  4.92 us

profile of v1, /device:TPU:7, one launch (start us, length us, event | category | flops | bytes accessed | tf_op | source)
XLA Modules:
  0.0 118.8 jit_solution(16172211800582926114)
XLA Ops:
  0.6 0.0 copy-start.3
  0.6 0.7 copy-done.3
  1.3 0.0 copy-start
  1.3 1.2 %copy-done = f32[1,1,512,512]{3,2,1,0:T(8,128)S(1)} copy-done((f32[1,1,512,512]{3,2,1,0:T(8,128)S(1)}, f32[1,1,512,512]{3,2,1,0:T(8,128)}, u32[]{:S(2)}) %copy-start) | copy-done | bytes 1048600
  2.5 0.0 copy-start.1
  2.5 0.9 copy-done.1
  3.5 0.0 copy-start.2
  3.5 0.8 copy-done.2
  4.3 113.3 %level.1 = (f32[384,128]{1,0:T(8,128)S(1)}, f32[3,32,32]{2,1,0:T(8,128)S(1)}) custom-call(f32[512,512]{1,0:T(8,128)S(1)} %bitcast.4, f32[384,128]{1,0:T(8,128)S(1)} %bitcast.5, f32[3,32,32]{2,1,0:T(8,128)S(1)} %copy-done.2, s32[3,16]{1,0:T(4,128)S(1)} %bitcast.7), custom_call_target="tpu_custom_call" | custom-call | tf_op jit(solution)/shard_map/level/pallas_call | solution.py:356
  117.5 0.7 copy.10
  118.2 0.6 copy.11
Async XLA Ops:
  0.6 0.7 copy-start.3
  1.3 1.2 %copy-start = (f32[1,1,512,512]{3,2,1,0:T(8,128)S(1)}, f32[1,1,512,512]{3,2,1,0:T(8,128)}, u32[]{:S(2)}) copy-start(f32[1,1,512,512]{3,2,1,0:T(8,128)} %param.4) | copy-start | bytes 3145732
  2.5 0.9 copy-start.1
  3.5 0.8 copy-start.2

commit v2 on v1

v2 whole, which is shorter than its diff:
```python
import jax
import jax.numpy as jnp
from jax import lax
from jax.experimental import pallas as pl
from jax.experimental.pallas import tpu as pltpu
from jax.sharding import PartitionSpec as P

F32 = jnp.float32
BF16 = jnp.bfloat16
MESH = pl.DeviceIdType.MESH
ROWS = 32
NSUP = 3
WIDTH = 512
GRID = 16


def split(x):
    high = x.astype(BF16)
    return high, (x - high.astype(F32)).astype(BF16)


def dot(a, b):
    return jnp.dot(a, b, preferred_element_type=F32)


def passing(row, chunk):
    bit = chunk & 1
    turn = 2 * (((row >> 1) ^ (chunk >> 1)) & 1) + (((chunk >> 2) & 1) ^ bit)
    return row ^ (4 * turn + bit)


def landing(row, block, chunk):
    return row ^ (2 * (((block >> 3) ^ (chunk >> 3)) & 1))


def chunk_at(row, block):
    high = ((row >> 1) ^ (block >> 1)) & 1
    low = row & 1
    middle = ((row >> 3) ^ (block >> 3)) & 1
    third = ((row >> 2) ^ block ^ low) & 1
    return block ^ (8 * high + 4 * third + 2 * middle + low)


def pack(y, put):
    lane = lax.broadcasted_iota(jnp.int32, (8, 128), 1) >> 5
    for g in range(4):
        tiles = [y[8 * u : 8 * u + 8, 128 * g : 128 * g + 128] for u in range(4)]
        for h in range(4):
            out = None
            for u in range(4):
                by = (32 * (u - h)) % 128
                moved = pltpu.roll(tiles[u], by, 1) if by else tiles[u]
                out = moved if out is None else jnp.where(lane == u, moved, out)
            put(4 * g + h, out)


def kernel(
    a_hbm, l_hbm, piv_hbm, s_hbm,
    y_out, d_ref,
    a_in, l_in, piv_in, s_in, a_high, a_low, src, taken, xbuf, pbuf, rbuf, sbuf, xrec, ybuf,
    e1s, e1r, e2s, e2r,
    load_sem, a_send, a_recv, xg_send, xg_recv, rs_send, rs_recv, xs_send, xs_recv, yg_send, yg_recv,
    e1_send, e1_recv, e2_send, e2_recv,
):
    p = lax.axis_index("prow")
    q = lax.axis_index("pcol")
    z = q & 7
    far = q >> 3

    loads = [
        pltpu.make_async_copy(source, target, load_sem.at[n])
        for n, (source, target) in enumerate(((l_hbm, l_in), (a_hbm, a_in), (s_hbm, s_in), (piv_hbm, piv_in)))
    ]
    for load in loads:
        load.start()

    other = p ^ 1
    beside = p ^ 2
    above = (p + 4) & 15
    below = (p - 4) & 15
    z_up = (q & 8) + ((z + 1) & 7)
    z_down = (q & 8) + ((z - 1) & 7)
    across = q ^ 8

    taker = passing(p, q)
    keeps = taker == p
    block = taker
    target_row = landing(p, block, q)
    stays = block == q
    origin = chunk_at(p, q)
    origin_row = landing(p, q, origin)

    barrier = pltpu.get_barrier_semaphore()
    for device in ((other, q), (beside, q), (above, q), (below, q), (p, z_up), (p, z_down), (p, across)):
        pl.semaphore_signal(barrier, inc=1, device_id=device, device_id_type=MESH)

    @pl.when(jnp.logical_not(keeps))
    def _():
        pl.semaphore_signal(barrier, inc=1, device_id=(taker, q), device_id_type=MESH)

    @pl.when(jnp.logical_not(stays))
    def _():
        pl.semaphore_signal(barrier, inc=1, device_id=(target_row, block), device_id_type=MESH)

    @pl.when(origin != q)
    def _():
        pl.semaphore_signal(barrier, inc=1, device_id=(origin_row, origin), device_id_type=MESH)

    loads[0].wait()
    for k in range(NSUP):
        for g in range(4):
            src[k, :, 128 * g : 128 * g + 128] = l_in[pl.ds(4 * k + g, ROWS, stride=12), :]
    with jax.named_scope("barrier"):
        pl.semaphore_wait(
            barrier, jnp.where(keeps, 7, 8) + jnp.where(stays, 0, 1) + jnp.where(origin == q, 0, 1)
        )

    def remote(source, target, send, recv, device):
        return pltpu.make_async_remote_copy(
            src_ref=source, dst_ref=target, send_sem=send, recv_sem=recv, device_id=device, device_id_type=MESH
        )

    sends = []

    def go(copy):
        copy.start()
        sends.append(copy)

    opposite = (p + 8) & 15
    kinds = (p, beside, below, below ^ 2, above, above ^ 2, opposite, opposite ^ 2)
    kinds = kinds + tuple(kind ^ 1 for kind in kinds)

    class Gather:
        def __init__(self, buffer, slots, send, recv):
            self.buffer, self.send, self.recv = buffer, send, recv
            self.where = [pl.ds(pl.multiple_of(ROWS * slot, ROWS), ROWS) for slot in slots]

        def piece(self, k, kind):
            return self.buffer.at[k, self.where[kind], :]

        def push(self, k, kind, slot, as_kind, row):
            piece = self.piece(k, kind)
            go(remote(piece, piece, self.send.at[k, slot], self.recv.at[k, as_kind], (row, q)))

        def wait(self, k, kind):
            piece = self.piece(k, kind)
            remote(piece, piece, self.send.at[k, 0], self.recv.at[k, kind], (other, q)).wait_recv()

        def own(self, k):
            self.push(k, 0, 1, 1, beside)
            self.push(k, 0, 2, 2, above)
            self.push(k, 0, 3, 4, below)
            self.push(k, 0, 8, 8, other)

        def second(self, k):
            self.wait(k, 1)
            self.push(k, 1, 4, 3, above)
            self.push(k, 1, 5, 5, below)
            self.push(k, 1, 9, 9, other)

        def ring(self, k):
            self.wait(k, 2)
            self.push(k, 2, 6, 6, above)
            self.push(k, 2, 10, 10, other)
            self.wait(k, 4)
            self.push(k, 4, 12, 12, other)
            self.wait(k, 5)
            self.push(k, 5, 7, 7, below)
            self.push(k, 5, 13, 13, other)
            self.wait(k, 3)
            self.push(k, 3, 11, 11, other)

        def last(self, k):
            self.wait(k, 6)
            self.push(k, 6, 14, 14, other)
            self.wait(k, 7)
            self.push(k, 7, 15, 15, other)

        def rest(self, k):
            for kind in range(8, 16):
                self.wait(k, kind)

    gx = Gather(xbuf, [chunk_at(kind, q) for kind in kinds], xg_send, xg_recv)
    gy = Gather(ybuf, list(kinds), yg_send, yg_recv)

    def take_copy(k):
        return remote(src.at[k], taken.at[k], a_send.at[k], a_recv.at[k], (taker, q))

    def land_copy(k):
        rows = pl.ds(pl.multiple_of(ROWS * q, ROWS), ROWS)
        return remote(taken.at[k], xbuf.at[k, rows, :], xg_send.at[k, 0], xg_recv.at[k, 0], (target_row, block))

    for k in range(NSUP):

        @pl.when(jnp.logical_not(keeps))
        def _():
            take_copy(k).start()

        @pl.when(keeps)
        def _():
            taken[k] = src[k]

    def st_take(k):
        @pl.when(jnp.logical_not(keeps))
        def _():
            take_copy(k).wait_recv()

        @pl.when(jnp.logical_not(stays))
        def _():
            land_copy(k).start()

        @pl.when(stays)
        def _():
            xbuf[k, gx.where[0], :] = taken[k]

    def st_prepare(k):
        loads[1].wait()
        a_high[...], a_low[...] = split(a_in[...])
        for n in range(NSUP):

            def put(t, tile, n=n):
                e1s[t, 8 * n : 8 * n + 8, :] = tile

            pack(src[n], put)
        loads[2].wait()
        loads[3].wait()

    def st_own(k):
        @pl.when(origin != q)
        def _():
            gx.wait(k, 0)

        gx.own(k)

    down_steps = (4, 3)
    up_steps = (3, 4)
    steps = [[down_steps[h], up_steps[h]] for h in range(2)]

    def block_rows(h, d):
        return pl.ds(pl.multiple_of(256 * h + ROWS * d, ROWS), ROWS)

    def sent_block(h, way, t):
        left = steps[h][way] - t
        return (z - left) & 7 if way == 0 else (z + left) & 7

    def send_sum(k, h, way, t):
        go(
            remote(
                pbuf.at[k, block_rows(h, sent_block(h, way, t)), :],
                rbuf.at[k, h, way, t],
                rs_send.at[k, h, way, t],
                rs_recv.at[k, h, way, t],
                (p, z_down if way == 0 else z_up),
            )
        )

    def wait_sum(k, h, way, t):
        remote(
            rbuf.at[k, h, way, t], rbuf.at[k, h, way, t], rs_send.at[k, h, way, t], rs_recv.at[k, h, way, t], (p, z_up)
        ).wait_recv()

    def mask_of(k, index):
        return s_in[k, index].astype(F32)

    def st_product(k):
        gx.rest(k)
        x_high, x_low = split(xbuf[k] * mask_of(k, q))
        for m in range(4):
            at = slice(128 * m, 128 * m + 128)
            pbuf[k, at, :] = dot(a_high[at, :], x_high) + dot(a_high[at, :], x_low) + dot(a_low[at, :], x_high)
        for h in range(2):
            for way in range(2):
                send_sum(k, h, way, 0)

    def st_sum(k, t):
        for h in range(2):
            for way in range(2):
                last = steps[h][way] - 1
                if t > last:
                    continue
                wait_sum(k, h, way, t)
                if t < last:
                    rows = block_rows(h, sent_block(h, way, t + 1))
                    pbuf[k, rows, :] = pbuf[k, rows, :] + rbuf[k, h, way, t]
                    send_sum(k, h, way, t + 1)
        if t == 3:
            for h in range(2):
                total = pbuf[k, block_rows(h, z), :]
                for way in range(2):
                    total = total + rbuf[k, h, way, steps[h][way] - 1]
                sbuf[k, h] = total
            go(remote(sbuf.at[k, 1 - far], xrec.at[k], xs_send.at[k], xs_recv.at[k], (p, across)))

    def st_spread(k):
        def one(i, carry):
            t = (p + i) & 15
            remote(e1s.at[t], e1r.at[p], e1_send.at[t], e1_recv.at[p], (t, q)).start()
            return carry

        lax.fori_loop(1, GRID, one, 0)
        e1r[p] = e1s[p]

    def st_panel(k):
        remote(xrec.at[k], xrec.at[k], xs_send.at[k], xs_recv.at[k], (p, across)).wait_recv()
        y = (sbuf[k, far] + xrec[k]) * (-mask_of(k, p))
        ybuf[k, gy.where[0], :] = y
        for g in range(4):
            y_out[pl.ds(4 * k + g, ROWS, stride=12), :] = y[:, 128 * g : 128 * g + 128]
        gy.own(k)

    def st_spread_wait(k):
        def one(i, carry):
            t = (p + i) & 15
            remote(e1r.at[t], e1r.at[t], e1_send.at[t], e1_recv.at[t], (other, q)).wait_recv()
            return carry

        lax.fori_loop(1, GRID, one, 0)

    def st_diagonal(k):
        turned = e1r[:, 8 * k : 8 * k + 8, :].reshape(128, 128).T
        left = [split(turned[32 * u : 32 * u + 32, :]) for u in range(4)]
        gy.rest(k)
        y = ybuf[k].reshape(GRID, 4, 8, WIDTH)
        total = None
        for u in range(4):
            l_high, l_low = left[u]
            y_high, y_low = split(y[:, u].reshape(128, WIDTH))
            term = dot(l_high, y_high) + dot(l_high, y_low) + dot(l_low, y_high)
            total = term if total is None else total + term

        def put(t, tile):
            e2s[k, t] = tile

        pack(total, put)

        def one(i, carry):
            t = (q + i) & 15
            remote(e2s.at[k, t], e2r.at[k, q], e2_send.at[k, t], e2_recv.at[k, q], (p, t)).start()
            return carry

        lax.fori_loop(1, GRID, one, 0)
        e2r[k, q] = e2s[k, q]

    def st_result(k):
        def one(i, carry):
            t = (q + i) & 15
            remote(e2r.at[k, t], e2r.at[k, t], e2_send.at[k, t], e2_recv.at[k, t], (other, q)).wait_recv()
            return carry

        lax.fori_loop(1, GRID, one, 0)
        total = jnp.sum(e2r[k], axis=0)
        parts = [total] + [pltpu.roll(total, 128 - 32 * u, 1) for u in range(1, 4)]
        square = jnp.concatenate(parts, axis=0)
        d_ref[k] = piv_in[k] - square[:, :ROWS]

    events = [(-8, 0, "prepare", st_prepare)]
    for k in range(NSUP):
        events.append((-9 + k, k, "take", st_take))
        events.append((0 + 3 * k, k, "own", st_own))
        events.append((2.5 + 3 * k, k, "second", gx.second))
        events.append((5 + 4 * k, k, "ring", gx.ring))
        events.append((8 + 4 * k, k, "last", gx.last))
        events.append((10 + 4 * k, k, "product", st_product))
        for t in range(4):
            events.append((14 + 5 * (t + k) - 0.1 * k, k, f"sum{t}", lambda k, t=t: st_sum(k, t)))
        events.append((35 + 5 * k, k, "panel", st_panel))
        events.append((38 + 5 * k, k, "ysecond", gy.second))
        events.append((41 + 5 * k, k, "yring", gy.ring))
        events.append((44 + 5 * k, k, "ylast", gy.last))
        events.append((46 + 5 * k, k, "diagonal", st_diagonal))
        events.append((54 + 5 * k, k, "result", st_result))
    events.append((18.5, 0, "spread", st_spread))
    events.append((43.5, 0, "arrived", st_spread_wait))
    for _, k, name, stage in sorted(events, key=lambda e: e[0]):
        with jax.named_scope(f"{name}_{k}"):
            stage(k)

    for k in range(NSUP):

        @pl.when(jnp.logical_not(keeps))
        def _():
            take_copy(k).wait_send()

        @pl.when(jnp.logical_not(stays))
        def _():
            land_copy(k).wait_send()

        def one(i, carry, k=k):
            t = (q + i) & 15
            remote(e2s.at[k, t], e2s.at[k, t], e2_send.at[k, t], e2_recv.at[k, t], (other, q)).wait_send()
            return carry

        lax.fori_loop(1, GRID, one, 0)

    def one(i, carry):
        t = (p + i) & 15
        remote(e1s.at[t], e1s.at[t], e1_send.at[t], e1_recv.at[t], (other, q)).wait_send()
        return carry

    lax.fori_loop(1, GRID, one, 0)
    for copy in sends:
        copy.wait_send()


def body(ancestor_inverse, factor_panel, pivot_inverse, structure):
    vmem = pl.BlockSpec(memory_space=pltpu.VMEM)
    hbm = pl.BlockSpec(memory_space=pltpu.HBM)
    dma = pltpu.SemaphoreType.DMA
    panel, diagonal = pl.pallas_call(
        kernel,
        out_shape=(
            jax.ShapeDtypeStruct((ROWS * NSUP * 4, 128), F32),
            jax.ShapeDtypeStruct(pivot_inverse.shape, F32),
        ),
        in_specs=[hbm] * 4,
        out_specs=(vmem, vmem),
        scratch_shapes=[
            pltpu.VMEM((WIDTH, WIDTH), F32),
            pltpu.VMEM((ROWS * NSUP * 4, 128), F32),
            pltpu.VMEM((NSUP, ROWS, ROWS), F32),
            pltpu.SMEM((NSUP, GRID), jnp.int32),
            pltpu.VMEM((WIDTH, WIDTH), BF16),
            pltpu.VMEM((WIDTH, WIDTH), BF16),
            pltpu.VMEM((NSUP, ROWS, WIDTH), F32),
            pltpu.VMEM((NSUP, ROWS, WIDTH), F32),
            pltpu.VMEM((NSUP, WIDTH, WIDTH), F32),
            pltpu.VMEM((NSUP, WIDTH, WIDTH), F32),
            pltpu.VMEM((NSUP, 2, 2, 4, ROWS, WIDTH), F32),
            pltpu.VMEM((NSUP, 2, ROWS, WIDTH), F32),
            pltpu.VMEM((NSUP, ROWS, WIDTH), F32),
            pltpu.VMEM((NSUP, WIDTH, WIDTH), F32),
            pltpu.VMEM((GRID, NSUP * 8, 128), F32),
            pltpu.VMEM((GRID, NSUP * 8, 128), F32),
            pltpu.VMEM((NSUP, GRID, 8, 128), F32),
            pltpu.VMEM((NSUP, GRID, 8, 128), F32),
            dma((4,)),
            dma((NSUP,)),
            dma((NSUP,)),
            dma((NSUP, 16)),
            dma((NSUP, 16)),
            dma((NSUP, 2, 2, 4)),
            dma((NSUP, 2, 2, 4)),
            dma((NSUP,)),
            dma((NSUP,)),
            dma((NSUP, 16)),
            dma((NSUP, 16)),
            dma((GRID,)),
            dma((GRID,)),
            dma((NSUP, GRID)),
            dma((NSUP, GRID)),
        ],
        compiler_params=pltpu.CompilerParams(
            collective_id=0, has_side_effects=True, vmem_limit_bytes=40 * 1024 * 1024
        ),
        name="level",
    )(
        ancestor_inverse.reshape(WIDTH, WIDTH),
        factor_panel.reshape(ROWS * NSUP * 4, 128),
        pivot_inverse,
        structure.T,
    )
    return panel.reshape(ROWS, 1, NSUP, WIDTH), diagonal


def solution(mesh):
    return jax.shard_map(
        body,
        mesh=mesh,
        in_specs=(
            P("prow", "pcol", None, None),
            P("pcol", "prow", None, None),
            P(None, "prow", "pcol"),
            P(),
        ),
        out_specs=(P("pcol", "prow", None, None), P(None, "prow", "pcol")),
        check_vma=False,
    )
```

time: 119 us -> 106 us (0.89); the launches traced: 119 us -> 104 us
  Pallas kernels: 113 us -> 98.6 us
    pallas_call x1, Pallas kernels: 113 us -> 98.6 us  [body(): pl.pallas_call(kernel, out_shape=(jax.ShapeDtypeStruct((ROWS * NSUP * 4,...]
where the time goes in v2:
time: 106 us; the launch traced here: 104 us
  Pallas kernels  98.6 us (93%)
  local copies, waits for them, and re-layouts  4.92 us (5%)
    pallas_call x1, Pallas kernels, body(): pl.pallas_call(kernel, out_shape=(jax.ShapeDtypeStruct((ROWS * NSUP * 4,...  98.6 us
    unnamed x10, local copies, waits for them, and re-layouts  4.92 us

profile of v2, /device:TPU:7, one launch (start us, length us, event | category | flops | bytes accessed | tf_op | source)
XLA Modules:
  0.0 104.1 jit_solution(11242778088576579558)
XLA Ops:
  0.6 0.0 copy-start.3
  0.6 0.7 copy-done.3
  1.3 0.0 copy-start
  1.3 1.2 %copy-done = f32[1,1,512,512]{3,2,1,0:T(8,128)S(1)} copy-done((f32[1,1,512,512]{3,2,1,0:T(8,128)S(1)}, f32[1,1,512,512]{3,2,1,0:T(8,128)}, u32[]{:S(2)}) %copy-start) | copy-done | bytes 1048600
  2.5 0.0 copy-start.1
  2.5 0.9 copy-done.1
  3.5 0.0 copy-start.2
  3.5 0.8 copy-done.2
  4.3 98.6 %level.1 = (f32[384,128]{1,0:T(8,128)S(1)}, f32[3,32,32]{2,1,0:T(8,128)S(1)}) custom-call(f32[512,512]{1,0:T(8,128)S(1)} %bitcast.4, f32[384,128]{1,0:T(8,128)S(1)} %bitcast.5, f32[3,32,32]{2,1,0:T(8,128)S(1)} %copy-done.2, s32[3,16]{1,0:T(4,128)S(1)} %bitcast.7), custom_call_target="tpu_custom_call" | custom-call | tf_op jit(solution)/shard_map/level/pallas_call | solution.py:409
  102.8 0.7 copy.10
  103.5 0.6 copy.11
Async XLA Ops:
  0.6 0.7 copy-start.3
  1.3 1.2 %copy-start = (f32[1,1,512,512]{3,2,1,0:T(8,128)S(1)}, f32[1,1,512,512]{3,2,1,0:T(8,128)}, u32[]{:S(2)}) copy-start(f32[1,1,512,512]{3,2,1,0:T(8,128)} %param.4) | copy-start | bytes 3145732
  2.5 0.9 copy-start.1
  3.5 0.8 copy-start.2

commit v3 on v2

v3 whole, which is shorter than its diff:
```python
import jax
import jax.numpy as jnp
from jax import lax
from jax.experimental import pallas as pl
from jax.experimental.pallas import tpu as pltpu
from jax.sharding import PartitionSpec as P

F32 = jnp.float32
BF16 = jnp.bfloat16
MESH = pl.DeviceIdType.MESH
ROWS = 32
NSUP = 3
WIDTH = 512
GRID = 16
UNITS = 6
COLS = 256
IN_FLIGHT = 3
FIRST_ACROSS = (1, 3)


VMEM_LIMIT = 40 * 1024 * 1024


def plan():
    when = {("prepare", 0): -8.0}
    product = []
    for k in range(UNITS):
        when["take", k] = -9 + 0.1 * k
        when["own", k] = 1.6 * k
        when["second", k] = 1.6 * k + 0.8
        when["forward", k] = 4.5 + 2.9 * k
        when["product", k] = 6.5 + 2.9 * k
        product.append(7.2 + 2.9 * k)
    when["spread", 0] = product[-1] + 0.1
    ready, x_free = {}, 0.0
    for k in range(UNITS):
        ready[k] = product[k]
        if k in FIRST_ACROSS:
            x_free = max(x_free, product[k]) + 5.4
            ready[k] = x_free + 2.5
    waiting = sorted(range(UNITS), key=lambda k: ready[k])
    flying, free, ended = [], 0.0, {}
    while waiting or flying:
        while waiting and len(flying) < IN_FLIGHT:
            k = waiting.pop(0)
            start = max(ready[k], max(ended.values(), default=0.0) if len(ended) + len(flying) >= IN_FLIGHT else 0.0)
            when["launch", k] = start
            flying.append((start, k, 0))
        start, k, t = min(flying)
        flying.remove((start, k, t))
        free = max(free, start) + (0.7 if k in FIRST_ACROSS else 1.4)
        when[f"sum{t}", k] = free + 1.9
        if t < 3:
            flying.append((free + 1.9, k, t + 1))
        else:
            ended[k] = free + 1.9
    free, here = 0.0, {}
    for k in sorted(range(UNITS), key=lambda k: ended[k]):
        when["panel", k] = ended[k] + (0.1 if k in FIRST_ACROSS else 3.5)
        free = max(free, when["panel", k]) + 2.9
        here[k] = free + 3.5
    for n in range(NSUP):
        when["diagonal", n] = max(here[2 * n], here[2 * n + 1])
        when["result", n] = when["diagonal", n] + 7.5
    when["arrived", 0] = min(when["diagonal", n] for n in range(NSUP)) - 0.1
    return [event for event, _ in sorted(when.items(), key=lambda item: item[1])]


ORDER = plan()


def split(x):
    high = x.astype(BF16)
    return high, (x - high.astype(F32)).astype(BF16)


def dot(a, b):
    return jnp.dot(a, b, preferred_element_type=F32)


def passing(row, chunk):
    bit = chunk & 1
    turn = 2 * (((row >> 1) ^ (chunk >> 1)) & 1) + (((chunk >> 2) & 1) ^ bit)
    return row ^ (4 * turn + bit)


def landing(row, block, chunk):
    return row ^ (2 * (((block >> 3) ^ (chunk >> 3)) & 1))


def chunk_at(row, block):
    high = ((row >> 1) ^ (block >> 1)) & 1
    low = row & 1
    middle = ((row >> 3) ^ (block >> 3)) & 1
    third = ((row >> 2) ^ block ^ low) & 1
    return block ^ (8 * high + 4 * third + 2 * middle + low)


def pack(y, put):
    lane = lax.broadcasted_iota(jnp.int32, (8, 128), 1) >> 5
    for g in range(y.shape[1] // 128):
        tiles = [y[8 * u : 8 * u + 8, 128 * g : 128 * g + 128] for u in range(4)]
        for h in range(4):
            out = None
            for u in range(4):
                by = (32 * (u - h)) % 128
                moved = pltpu.roll(tiles[u], by, 1) if by else tiles[u]
                out = moved if out is None else jnp.where(lane == u, moved, out)
            put(4 * g + h, out)


def kernel(
    a_hbm, l_hbm, piv_hbm, s_hbm,
    y_out, d_out,
    a_in, l_in, piv_in, s_in, a_high, a_low, src, taken, xbuf, pbuf, rbuf, sbuf, xrec, xhalf, ybuf,
    e1s, e1r, e2s, e2r,
    load_sem, a_send, a_recv, xg_send, xg_recv, rs_send, rs_recv, xs_send, xs_recv, yg_send, yg_recv,
    e1_send, e1_recv, e2_send, e2_recv,
):
    p = lax.axis_index("prow")
    q = lax.axis_index("pcol")
    z = q & 7
    far = q >> 3

    loads = [
        pltpu.make_async_copy(source, target, load_sem.at[n])
        for n, (source, target) in enumerate(((l_hbm, l_in), (a_hbm, a_in), (s_hbm, s_in), (piv_hbm, piv_in)))
    ]
    for load in loads:
        load.start()

    other = p ^ 1
    beside = p ^ 2
    above = (p + 4) & 15
    below = (p - 4) & 15
    z_up = (q & 8) + ((z + 1) & 7)
    z_down = (q & 8) + ((z - 1) & 7)
    across = q ^ 8

    taker = passing(p, q)
    keeps = taker == p
    block = taker
    target_row = landing(p, block, q)
    stays = block == q
    origin = chunk_at(p, q)
    origin_row = landing(p, q, origin)
    second = chunk_at(beside, q)
    second_row = landing(beside, q, second)

    barrier = pltpu.get_barrier_semaphore()
    opposite = (p + 8) & 15
    for device in (
        (other, q), (beside, q), (above, q), (below, q), (opposite, q), (p, z_up), (p, z_down), (p, across)
    ):
        pl.semaphore_signal(barrier, inc=1, device_id=device, device_id_type=MESH)

    @pl.when(jnp.logical_not(keeps))
    def _():
        pl.semaphore_signal(barrier, inc=1, device_id=(taker, q), device_id_type=MESH)

    @pl.when(jnp.logical_not(stays))
    def _():
        pl.semaphore_signal(barrier, inc=1, device_id=(target_row, block), device_id_type=MESH)

    @pl.when(origin != q)
    def _():
        pl.semaphore_signal(barrier, inc=1, device_id=(origin_row, origin), device_id_type=MESH)

    pl.semaphore_signal(barrier, inc=1, device_id=(target_row ^ 2, block), device_id_type=MESH)
    pl.semaphore_signal(barrier, inc=1, device_id=(second_row, second), device_id_type=MESH)

    loads[0].wait()
    for u in range(UNITS):
        for g in range(2):
            src[u, :, 128 * g : 128 * g + 128] = l_in[pl.ds(2 * u + g, ROWS, stride=12), :]
    with jax.named_scope("barrier"):
        pl.semaphore_wait(
            barrier, jnp.where(keeps, 10, 11) + jnp.where(stays, 0, 1) + jnp.where(origin == q, 0, 1)
        )

    def remote(source, target, send, recv, device):
        return pltpu.make_async_remote_copy(
            src_ref=source, dst_ref=target, send_sem=send, recv_sem=recv, device_id=device, device_id_type=MESH
        )

    sends = []

    def go(copy):
        copy.start()
        sends.append(copy)

    kinds = (p, beside, below, below ^ 2, above, above ^ 2, opposite, opposite ^ 2)
    kinds = kinds + tuple(kind ^ 1 for kind in kinds)

    where = [pl.ds(pl.multiple_of(ROWS * chunk_at(kind, q), ROWS), ROWS) for kind in kinds]

    def piece(k, kind):
        return xbuf.at[k, where[kind], :]

    def push(k, kind, slot, as_kind, row):
        go(remote(piece(k, kind), piece(k, kind), xg_send.at[k, slot], xg_recv.at[k, as_kind], (row, q)))

    def wait_piece(k, kind):
        remote(piece(k, kind), piece(k, kind), xg_send.at[k, 0], xg_recv.at[k, kind], (other, q)).wait_recv()

    def push_all(k, kind):
        push(k, kind, 2 + kind, 2 + kind, above)
        push(k, kind, 4 + kind, 4 + kind, below)
        push(k, kind, 6 + kind, 6 + kind, opposite)
        push(k, kind, 8 + kind, 8 + kind, other)

    def take_copy(k):
        return remote(src.at[k], taken.at[k], a_send.at[k], a_recv.at[k], (taker, q))

    def land_copy(k, aside):
        rows = pl.ds(pl.multiple_of(ROWS * q, ROWS), ROWS)
        return remote(
            taken.at[k],
            xbuf.at[k, rows, :],
            xg_send.at[k, aside],
            xg_recv.at[k, aside],
            (target_row ^ (2 * aside), block),
        )

    for k in range(UNITS):

        @pl.when(jnp.logical_not(keeps))
        def _():
            take_copy(k).start()

        @pl.when(keeps)
        def _():
            taken[k] = src[k]

    def st_take(k):
        @pl.when(jnp.logical_not(keeps))
        def _():
            take_copy(k).wait_recv()

        @pl.when(jnp.logical_not(stays))
        def _():
            land_copy(k, 0).start()

        go(land_copy(k, 1))

        @pl.when(stays)
        def _():
            xbuf[k, where[0], :] = taken[k]

    def st_prepare(k):
        loads[1].wait()
        a_high[...], a_low[...] = split(a_in[...])
        for n in range(NSUP):

            for h in range(2):

                def put(t, tile, n=n, h=h):
                    e1s[8 * h + t, 8 * n : 8 * n + 8, :] = tile

                pack(src[2 * n + h], put)
        loads[2].wait()
        loads[3].wait()

    def st_own(k):
        @pl.when(origin != q)
        def _():
            wait_piece(k, 0)

        push_all(k, 0)

    def st_second(k):
        wait_piece(k, 1)
        push_all(k, 1)

    def st_forward(k):
        for kind in (2, 4, 3, 5, 6, 7):
            wait_piece(k, kind)
            push(k, kind, 8 + kind, 8 + kind, other)

    across_first = FIRST_ACROSS
    halves = [(0,) if k in across_first else (0, 1) for k in range(UNITS)]

    def steps(k, h, way):
        return 4 if (k + h + way) % 2 == 0 else 3

    def block_rows(k, h, d):
        half = far if k in across_first else h
        return pl.ds(pl.multiple_of(256 * half + ROWS * d, ROWS), ROWS)

    def sent_block(k, h, way, t):
        left = steps(k, h, way) - t
        return (z - left) & 7 if way == 0 else (z + left) & 7

    def send_sum(k, h, way, t):
        go(
            remote(
                pbuf.at[k, block_rows(k, h, sent_block(k, h, way, t)), :],
                rbuf.at[k, h, way, t],
                rs_send.at[k, h, way, t],
                rs_recv.at[k, h, way, t],
                (p, z_down if way == 0 else z_up),
            )
        )

    def wait_sum(k, h, way, t):
        remote(
            rbuf.at[k, h, way, t], rbuf.at[k, h, way, t], rs_send.at[k, h, way, t], rs_recv.at[k, h, way, t], (p, z_up)
        ).wait_recv()

    def mask_of(k, index):
        return s_in[k // 2, index].astype(F32)

    def half_copy(k):
        rows = pl.ds(pl.multiple_of(256 * (1 - far), 256), 256)
        at = across_first.index(k)
        return remote(pbuf.at[k, rows, :], xhalf.at[at], xs_send.at[k], xs_recv.at[k], (p, across))

    def st_product(k):
        for kind in range(8, 16):
            wait_piece(k, kind)
        x_high, x_low = split(xbuf[k] * mask_of(k, q))
        for m in range(4):
            at = slice(128 * m, 128 * m + 128)
            pbuf[k, at, :] = dot(a_high[at, :], x_high) + dot(a_high[at, :], x_low) + dot(a_low[at, :], x_high)
        if k in across_first:
            go(half_copy(k))

    def st_launch(k):
        if k in across_first:
            half_copy(k).wait_recv()
            rows = pl.ds(pl.multiple_of(256 * far, 256), 256)
            pbuf[k, rows, :] = pbuf[k, rows, :] + xhalf[across_first.index(k)]
        for h in halves[k]:
            for way in range(2):
                send_sum(k, h, way, 0)

    def st_sum(k, t):
        for h in halves[k]:
            for way in range(2):
                last = steps(k, h, way) - 1
                if t > last:
                    continue
                wait_sum(k, h, way, t)
                if t < last:
                    rows = block_rows(k, h, sent_block(k, h, way, t + 1))
                    pbuf[k, rows, :] = pbuf[k, rows, :] + rbuf[k, h, way, t]
                    send_sum(k, h, way, t + 1)
        if t == 3:
            for h in halves[k]:
                total = pbuf[k, block_rows(k, h, z), :]
                for way in range(2):
                    total = total + rbuf[k, h, way, steps(k, h, way) - 1]
                sbuf[k, h] = total
            if k not in across_first:
                go(remote(sbuf.at[k, 1 - far], xrec.at[k], xs_send.at[k], xs_recv.at[k], (p, across)))

    core = p & 1
    pair = p - core

    def spread_copy(t):
        tiles = pl.ds(2 * (t >> 1), 2)
        return remote(e1s.at[tiles], e1r.at[p], e1_send.at[t], e1_recv.at[p], (t, q))

    def st_spread(k):
        def one(i, carry):
            spread_copy((p + i) & 15).start()
            return carry

        lax.fori_loop(1, GRID, one, 0)
        e1r[p] = e1s[pl.ds(pair, 2)]

    y_rows = pl.ds(pl.multiple_of(ROWS * p, ROWS), ROWS)

    def y_copy(k, row, slot):
        return remote(ybuf.at[k, y_rows, :], ybuf.at[k, y_rows, :], yg_send.at[k, slot], yg_recv.at[k, p], (row, q))

    def st_panel(k):
        if k in across_first:
            total = sbuf[k, 0]
        else:
            remote(xrec.at[k], xrec.at[k], xs_send.at[k], xs_recv.at[k], (p, across)).wait_recv()
            total = sbuf[k, far] + xrec[k]
        y = total * (-mask_of(k, p))
        ybuf[k, y_rows, :] = y
        for g in range(2):
            y_out[pl.ds(2 * k + g, ROWS, stride=12), :] = y[:, 128 * g : 128 * g + 128]
        near = p - core + k % 2
        for n, turn in enumerate((2, 4, 12, 6, 14, 8, 10)):
            row = (near ^ (turn & 2)) + (turn & 12) & 15
            go(y_copy(k, row, n + 1))

        @pl.when(core != k % 2)
        def _():
            y_copy(k, other, 0).start()

    def st_spread_wait(k):
        def one(i, carry):
            t = (p + i) & 15
            remote(e1r.at[t], e1r.at[t], e1_send.at[t], e1_recv.at[t], (other, q)).wait_recv()
            return carry

        lax.fori_loop(1, GRID, one, 0)

    def e2_copy(n, w, t):
        column = 8 * core + t
        return remote(
            e2s.at[n, w, t], e2r.at[n, q], e2_send.at[n, w, t], e2_recv.at[n, q], (pair + w, column)
        )

    def elsewhere(w, t):
        return jnp.logical_or(pair + w != p, 8 * core + t != q)

    def st_diagonal(n):
        left = []
        for w in range(2):
            turned = e1r[:, w, 8 * n : 8 * n + 8, :].reshape(128, 128).T
            left.append([turned[32 * u : 32 * u + 32, :] for u in range(4)])
        left = [split(jnp.concatenate([left[0][u], left[1][u]], axis=0)) for u in range(4)]
        unit = 2 * n + core

        def one(i, carry):
            row = (p + i) & 15
            rows = pl.ds(pl.multiple_of(ROWS * row, ROWS), ROWS)
            piece = ybuf.at[unit, rows, :]
            remote(piece, piece, yg_send.at[n, 0], yg_recv.at[unit, row], (other, q)).wait_recv()
            return carry

        lax.fori_loop(1, GRID, one, 0)
        y = ybuf[unit].reshape(GRID, 4, 8, COLS)
        total = None
        for u in range(4):
            l_high, l_low = left[u]
            y_high, y_low = split(y[:, u].reshape(128, COLS))
            term = dot(l_high, y_high) + dot(l_high, y_low) + dot(l_low, y_high)
            total = term if total is None else total + term
        for w in range(2):

            def put(t, tile, w=w):
                e2s[n, w, t] = tile

            pack(total[32 * w : 32 * w + 32, :], put)

        def two(i, carry):
            t = (q + i) & 7
            for w in range(2):

                @pl.when(elsewhere(w, t))
                def _():
                    e2_copy(n, w, t).start()

            return carry

        lax.fori_loop(0, 8, two, 0)

        @pl.when(far == core)
        def _():
            e2r[n, q] = e2s[n, core, q & 7]

    def st_result(n):
        def one(i, carry):
            t = (q + i) & 15

            @pl.when(jnp.logical_or(t != q, far != core))
            def _():
                remote(e2r.at[n, t], e2r.at[n, t], e1_send.at[0], e2_recv.at[n, t], (other, q)).wait_recv()

            return carry

        lax.fori_loop(0, GRID, one, 0)
        total = jnp.sum(e2r[n], axis=0)
        parts = [total] + [pltpu.roll(total, 128 - 32 * u, 1) for u in range(1, 4)]
        square = jnp.concatenate(parts, axis=0)
        d_out[n] = piv_in[n] - square[:, :ROWS]

    stages = {
        "take": st_take,
        "prepare": st_prepare,
        "own": st_own,
        "second": st_second,
        "forward": st_forward,
        "product": st_product,
        "launch": st_launch,
        "panel": st_panel,
        "spread": st_spread,
        "arrived": st_spread_wait,
        "diagonal": st_diagonal,
        "result": st_result,
    }
    for t in range(4):
        stages[f"sum{t}"] = lambda k, t=t: st_sum(k, t)
    for name, k in ORDER:
        with jax.named_scope(f"{name}_{k}"):
            stages[name](k)

    for k in range(UNITS):

        @pl.when(jnp.logical_not(keeps))
        def _():
            take_copy(k).wait_send()

        @pl.when(jnp.logical_not(stays))
        def _():
            land_copy(k, 0).wait_send()

        @pl.when(core != k % 2)
        def _():
            y_copy(k, other, 0).wait_send()

    for n in range(NSUP):

        def two(t, carry, n=n):
            for w in range(2):

                @pl.when(elsewhere(w, t))
                def _():
                    e2_copy(n, w, t).wait_send()

            return carry

        lax.fori_loop(0, 8, two, 0)

    def one(i, carry):
        spread_copy((p + i) & 15).wait_send()
        return carry

    lax.fori_loop(1, GRID, one, 0)
    for copy in sends:
        copy.wait_send()


def body(ancestor_inverse, factor_panel, pivot_inverse, structure):
    hbm = pl.BlockSpec(memory_space=pltpu.HBM)
    dma = pltpu.SemaphoreType.DMA
    panel, diagonal = pl.pallas_call(
        kernel,
        out_shape=(
            pltpu.VMEM((ROWS * NSUP * 4, 128), F32),
            pltpu.VMEM(pivot_inverse.shape, F32),
        ),
        in_specs=[hbm] * 4,
        out_specs=(pl.BlockSpec(memory_space=pltpu.VMEM),)*2,
        scratch_shapes=[
            pltpu.VMEM((WIDTH, WIDTH), F32),
            pltpu.VMEM((ROWS * NSUP * 4, 128), F32),
            pltpu.VMEM((NSUP, ROWS, ROWS), F32),
            pltpu.SMEM((NSUP, GRID), jnp.int32),
            pltpu.VMEM((WIDTH, WIDTH), BF16),
            pltpu.VMEM((WIDTH, WIDTH), BF16),
            pltpu.VMEM((UNITS, ROWS, COLS), F32),
            pltpu.VMEM((UNITS, ROWS, COLS), F32),
            pltpu.VMEM((UNITS, WIDTH, COLS), F32),
            pltpu.VMEM((UNITS, WIDTH, COLS), F32),
            pltpu.VMEM((UNITS, 2, 2, 4, ROWS, COLS), F32),
            pltpu.VMEM((UNITS, 2, ROWS, COLS), F32),
            pltpu.VMEM((UNITS, ROWS, COLS), F32),
            pltpu.VMEM((len(FIRST_ACROSS), 256, COLS), F32),
            pltpu.VMEM((UNITS, WIDTH, COLS), F32),
            pltpu.VMEM((GRID, NSUP * 8, 128), F32),
            pltpu.VMEM((GRID, 2, NSUP * 8, 128), F32),
            pltpu.VMEM((NSUP, 2, 8, 8, 128), F32),
            pltpu.VMEM((NSUP, GRID, 8, 128), F32),
            dma((4,)),
            dma((UNITS,)),
            dma((UNITS,)),
            dma((UNITS, 16)),
            dma((UNITS, 16)),
            dma((UNITS, 2, 2, 4)),
            dma((UNITS, 2, 2, 4)),
            dma((UNITS,)),
            dma((UNITS,)),
            dma((UNITS, 8)),
            dma((UNITS, GRID)),
            dma((GRID,)),
            dma((GRID,)),
            dma((NSUP, 2, 8)),
            dma((NSUP, GRID)),
        ],
        compiler_params=pltpu.CompilerParams(
            collective_id=0, has_side_effects=True, vmem_limit_bytes=VMEM_LIMIT
        ),
        name="level",
    )(
        pltpu.with_memory_space_constraint(ancestor_inverse.reshape(WIDTH, WIDTH), pltpu.HBM),
        pltpu.with_memory_space_constraint(factor_panel.reshape(ROWS * NSUP * 4, 128), pltpu.HBM),
        pltpu.with_memory_space_constraint(pivot_inverse, pltpu.HBM),
        pltpu.with_memory_space_constraint(structure.T, pltpu.HBM),
    )
    return panel.reshape(ROWS, 1, NSUP, WIDTH), diagonal


def solution(mesh):
    return jax.shard_map(
        body,
        mesh=mesh,
        in_specs=(
            P("prow", "pcol", None, None),
            P("pcol", "prow", None, None),
            P(None, "prow", "pcol"),
            P(),
        ),
        out_specs=(P("pcol", "prow", None, None), P(None, "prow", "pcol")),
        check_vma=False,
    )
```

time: 106 us -> 91.1 us (0.86); the launches traced: 104 us -> 91 us
  Pallas kernels: 98.6 us -> 89 us
  local copies, waits for them, and re-layouts: 4.92 us -> 1.3 us
    pallas_call x1, Pallas kernels: 98.6 us -> 89 us  [body(): pl.pallas_call(kernel, out_shape=(pltpu.VMEM((ROWS * NSUP * 4, 128), F32)...]
    unnamed x10 -> x2, local copies, waits for them, and re-layouts: 4.92 us -> 1.3 us
where the time goes in v3:
time: 91.1 us; the launch traced here: 91 us
  Pallas kernels  89 us (98%)
  local copies, waits for them, and re-layouts  1.3 us (1%)
    pallas_call x1, Pallas kernels, body(): pl.pallas_call(kernel, out_shape=(pltpu.VMEM((ROWS * NSUP * 4, 128), F32)...  89 us

profile of v3, /device:TPU:7, one launch (start us, length us, event | category | flops | bytes accessed | tf_op | source)
XLA Modules:
  0.0 91.0 jit_solution(15196227557438395648)
XLA Ops:
  0.6 89.0 %level.1 = (f32[384,128]{1,0:T(8,128)S(1)}, f32[3,32,32]{2,1,0:T(8,128)S(1)}) custom-call(f32[512,512]{1,0:T(8,128)} %bitcast.5, f32[384,128]{1,0:T(8,128)} %bitcast.6, f32[3,32,32]{2,1,0:T(8,128)} %piv_hbm.1, s32[3,16]{1,0:T(4,128)} %bitcast.7), custom_call_target="tpu_custom_call" | custom-call | tf_op jit(solution)/shard_map/level/pallas_call | solution.py:534
  89.7 0.7 copy.10
  90.4 0.6 copy.11

commit v4 on v3

--- a/solution.py
+++ b/solution.py
@@ -15,58 +15,25 @@
 UNITS = 6
 COLS = 256
 IN_FLIGHT = 3
-FIRST_ACROSS = (1, 3)
+FIRST_ACROSS = ()
 
 
 VMEM_LIMIT = 40 * 1024 * 1024
 
 
-def plan():
-    when = {("prepare", 0): -8.0}
-    product = []
-    for k in range(UNITS):
-        when["take", k] = -9 + 0.1 * k
-        when["own", k] = 1.6 * k
-        when["second", k] = 1.6 * k + 0.8
-        when["forward", k] = 4.5 + 2.9 * k
-        when["product", k] = 6.5 + 2.9 * k
-        product.append(7.2 + 2.9 * k)
-    when["spread", 0] = product[-1] + 0.1
-    ready, x_free = {}, 0.0
-    for k in range(UNITS):
-        ready[k] = product[k]
-        if k in FIRST_ACROSS:
-            x_free = max(x_free, product[k]) + 5.4
-            ready[k] = x_free + 2.5
-    waiting = sorted(range(UNITS), key=lambda k: ready[k])
-    flying, free, ended = [], 0.0, {}
-    while waiting or flying:
-        while waiting and len(flying) < IN_FLIGHT:
-            k = waiting.pop(0)
-            start = max(ready[k], max(ended.values(), default=0.0) if len(ended) + len(flying) >= IN_FLIGHT else 0.0)
-            when["launch", k] = start
-            flying.append((start, k, 0))
-        start, k, t = min(flying)
-        flying.remove((start, k, t))
-        free = max(free, start) + (0.7 if k in FIRST_ACROSS else 1.4)
-        when[f"sum{t}", k] = free + 1.9
-        if t < 3:
-            flying.append((free + 1.9, k, t + 1))
-        else:
-            ended[k] = free + 1.9
-    free, here = 0.0, {}
-    for k in sorted(range(UNITS), key=lambda k: ended[k]):
-        when["panel", k] = ended[k] + (0.1 if k in FIRST_ACROSS else 3.5)
-        free = max(free, when["panel", k]) + 2.9
-        here[k] = free + 3.5
-    for n in range(NSUP):
-        when["diagonal", n] = max(here[2 * n], here[2 * n + 1])
-        when["result", n] = when["diagonal", n] + 7.5
-    when["arrived", 0] = min(when["diagonal", n] for n in range(NSUP)) - 0.1
-    return [event for event, _ in sorted(when.items(), key=lambda item: item[1])]
-
-
-ORDER = plan()
+ORDER = (
+    ("take", 0), ("prepare", 0), ("take", 1), ("take", 2), ("take", 3), ("take", 4), ("take", 5), ("own", 0),
+    ("second", 0), ("own", 1), ("second", 1), ("own", 2), ("second", 2), ("own", 3), ("second", 3),
+    ("forward", 0), ("own", 4), ("second", 4), ("product", 0), ("own", 5), ("launch", 0), ("second", 5),
+    ("forward", 1), ("product", 1), ("launch", 1), ("forward", 2), ("sum0", 0), ("product", 2), ("launch", 2),
+    ("forward", 3), ("sum0", 1), ("sum1", 0), ("product", 3), ("launch", 3), ("forward", 4), ("sum0", 2),
+    ("sum1", 1), ("product", 4), ("forward", 5), ("sum2", 0), ("sum0", 3), ("product", 5), ("spread", 0),
+    ("sum1", 2), ("sum2", 1), ("sum3", 0), ("launch", 4), ("sum1", 3), ("sum2", 2), ("sum3", 1),
+    ("launch", 5), ("panel", 0), ("sum0", 4), ("sum2", 3), ("sum3", 2), ("panel", 1), ("sum0", 5),
+    ("sum1", 4), ("sum3", 3), ("panel", 2), ("sum1", 5), ("sum2", 4), ("panel", 3), ("arrived", 0),
+    ("diagonal", 0), ("sum3", 4), ("sum2", 5), ("sum3", 5), ("panel", 4), ("diagonal", 1), ("panel", 5),
+    ("drain", 0), ("diagonal", 2), ("drain", 1), ("result", 0), ("result", 1), ("result", 2),
+)
 
 
 def split(x):
@@ -114,7 +81,7 @@
     y_out, d_out,
     a_in, l_in, piv_in, s_in, a_high, a_low, src, taken, xbuf, pbuf, rbuf, sbuf, xrec, xhalf, ybuf,
     e1s, e1r, e2s, e2r,
-    load_sem, a_send, a_recv, xg_send, xg_recv, rs_send, rs_recv, xs_send, xs_recv, yg_send, yg_recv,
+    load_sem, a_send, a_recv, land_send, xg_send, xg_recv, rs_send, rs_recv, xs_send, xs_recv, yg_send, yg_recv,
     e1_send, e1_recv, e2_send, e2_recv,
 ):
     p = lax.axis_index("prow")
@@ -178,17 +145,20 @@
             barrier, jnp.where(keeps, 10, 11) + jnp.where(stays, 0, 1) + jnp.where(origin == q, 0, 1)
         )
 
+    def start(copy):
+        copy.start()
+
+    def came(ref, sem):
+        remote(ref, ref, sem, sem, (other, q)).wait_recv()
+
+    def went(ref, sem):
+        remote(ref, ref, sem, sem, (other, q)).wait_send()
+
     def remote(source, target, send, recv, device):
         return pltpu.make_async_remote_copy(
             src_ref=source, dst_ref=target, send_sem=send, recv_sem=recv, device_id=device, device_id_type=MESH
         )
 
-    sends = []
-
-    def go(copy):
-        copy.start()
-        sends.append(copy)
-
     kinds = (p, beside, below, below ^ 2, above, above ^ 2, opposite, opposite ^ 2)
     kinds = kinds + tuple(kind ^ 1 for kind in kinds)
 
@@ -197,27 +167,28 @@
     def piece(k, kind):
         return xbuf.at[k, where[kind], :]
 
-    def push(k, kind, slot, as_kind, row):
-        go(remote(piece(k, kind), piece(k, kind), xg_send.at[k, slot], xg_recv.at[k, as_kind], (row, q)))
-
-    def wait_piece(k, kind):
-        remote(piece(k, kind), piece(k, kind), xg_send.at[k, 0], xg_recv.at[k, kind], (other, q)).wait_recv()
+    def push(k, kind, as_kind, row):
+        group = as_kind if as_kind < 2 else 2 if as_kind < 6 else 3 if as_kind < 8 else 4
+        start(remote(piece(k, kind), piece(k, kind), xg_send.at[0], xg_recv.at[k, group], (row, q)))
+
+    def pieces(k, count):
+        return xbuf.at[k, pl.ds(0, ROWS * count), :]
 
     def push_all(k, kind):
-        push(k, kind, 2 + kind, 2 + kind, above)
-        push(k, kind, 4 + kind, 4 + kind, below)
-        push(k, kind, 6 + kind, 6 + kind, opposite)
-        push(k, kind, 8 + kind, 8 + kind, other)
+        push(k, kind, 2 + kind, above)
+        push(k, kind, 4 + kind, below)
+        push(k, kind, 6 + kind, opposite)
+        push(k, kind, 8 + kind, other)
 
     def take_copy(k):
-        return remote(src.at[k], taken.at[k], a_send.at[k], a_recv.at[k], (taker, q))
+        return remote(src.at[k], taken.at[k], a_send.at[0], a_recv.at[k], (taker, q))
 
     def land_copy(k, aside):
         rows = pl.ds(pl.multiple_of(ROWS * q, ROWS), ROWS)
         return remote(
             taken.at[k],
             xbuf.at[k, rows, :],
-            xg_send.at[k, aside],
+            land_send.at[0] if aside == 0 else xg_send.at[0],
             xg_recv.at[k, aside],
             (target_row ^ (2 * aside), block),
         )
@@ -241,7 +212,7 @@
         def _():
             land_copy(k, 0).start()
 
-        go(land_copy(k, 1))
+        land_copy(k, 1).start()
 
         @pl.when(stays)
         def _():
@@ -264,18 +235,21 @@
     def st_own(k):
         @pl.when(origin != q)
         def _():
-            wait_piece(k, 0)
+            came(pieces(k, 1), xg_recv.at[k, 0])
 
         push_all(k, 0)
 
     def st_second(k):
-        wait_piece(k, 1)
+        came(pieces(k, 1), xg_recv.at[k, 1])
         push_all(k, 1)
 
     def st_forward(k):
-        for kind in (2, 4, 3, 5, 6, 7):
-            wait_piece(k, kind)
-            push(k, kind, 8 + kind, 8 + kind, other)
+        came(pieces(k, 4), xg_recv.at[k, 2])
+        for kind in range(2, 6):
+            push(k, kind, 8 + kind, other)
+        came(pieces(k, 2), xg_recv.at[k, 3])
+        for kind in range(6, 8):
+            push(k, kind, 8 + kind, other)
 
     across_first = FIRST_ACROSS
     halves = [(0,) if k in across_first else (0, 1) for k in range(UNITS)]
@@ -291,21 +265,19 @@
         left = steps(k, h, way) - t
         return (z - left) & 7 if way == 0 else (z + left) & 7
 
+    def slot(t, way):
+        return 2 * t + way if t < 3 else 6
+
     def send_sum(k, h, way, t):
-        go(
+        start(
             remote(
                 pbuf.at[k, block_rows(k, h, sent_block(k, h, way, t)), :],
-                rbuf.at[k, h, way, t],
-                rs_send.at[k, h, way, t],
-                rs_recv.at[k, h, way, t],
+                rbuf.at[k, h, slot(t, way)],
+                rs_send.at[k],
+                rs_recv.at[k, h, t],
                 (p, z_down if way == 0 else z_up),
             )
         )
-
-    def wait_sum(k, h, way, t):
-        remote(
-            rbuf.at[k, h, way, t], rbuf.at[k, h, way, t], rs_send.at[k, h, way, t], rs_recv.at[k, h, way, t], (p, z_up)
-        ).wait_recv()
 
     def mask_of(k, index):
         return s_in[k // 2, index].astype(F32)
@@ -316,14 +288,13 @@
         return remote(pbuf.at[k, rows, :], xhalf.at[at], xs_send.at[k], xs_recv.at[k], (p, across))
 
     def st_product(k):
-        for kind in range(8, 16):
-            wait_piece(k, kind)
+        came(pieces(k, 8), xg_recv.at[k, 4])
         x_high, x_low = split(xbuf[k] * mask_of(k, q))
         for m in range(4):
             at = slice(128 * m, 128 * m + 128)
             pbuf[k, at, :] = dot(a_high[at, :], x_high) + dot(a_high[at, :], x_low) + dot(a_low[at, :], x_high)
         if k in across_first:
-            go(half_copy(k))
+            half_copy(k).start()
 
     def st_launch(k):
         if k in across_first:
@@ -336,30 +307,27 @@
 
     def st_sum(k, t):
         for h in halves[k]:
+            came(rbuf.at[k, h, pl.ds(2 * t, 2 if t < 3 else 1)], rs_recv.at[k, h, t])
             for way in range(2):
-                last = steps(k, h, way) - 1
-                if t > last:
-                    continue
-                wait_sum(k, h, way, t)
-                if t < last:
+                if t < steps(k, h, way) - 1:
                     rows = block_rows(k, h, sent_block(k, h, way, t + 1))
-                    pbuf[k, rows, :] = pbuf[k, rows, :] + rbuf[k, h, way, t]
+                    pbuf[k, rows, :] = pbuf[k, rows, :] + rbuf[k, h, slot(t, way)]
                     send_sum(k, h, way, t + 1)
         if t == 3:
             for h in halves[k]:
                 total = pbuf[k, block_rows(k, h, z), :]
                 for way in range(2):
-                    total = total + rbuf[k, h, way, steps(k, h, way) - 1]
+                    total = total + rbuf[k, h, slot(steps(k, h, way) - 1, way)]
                 sbuf[k, h] = total
             if k not in across_first:
-                go(remote(sbuf.at[k, 1 - far], xrec.at[k], xs_send.at[k], xs_recv.at[k], (p, across)))
+                start(remote(sbuf.at[k, 1 - far], xrec.at[k], xs_send.at[k], xs_recv.at[k], (p, across)))
 
     core = p & 1
     pair = p - core
 
     def spread_copy(t):
         tiles = pl.ds(2 * (t >> 1), 2)
-        return remote(e1s.at[tiles], e1r.at[p], e1_send.at[t], e1_recv.at[p], (t, q))
+        return remote(e1s.at[tiles], e1r.at[p], e1_send.at[0], e1_recv.at[0], (t, q))
 
     def st_spread(k):
         def one(i, carry):
@@ -371,40 +339,35 @@
 
     y_rows = pl.ds(pl.multiple_of(ROWS * p, ROWS), ROWS)
 
-    def y_copy(k, row, slot):
-        return remote(ybuf.at[k, y_rows, :], ybuf.at[k, y_rows, :], yg_send.at[k, slot], yg_recv.at[k, p], (row, q))
+    def y_copy(k, row):
+        return remote(ybuf.at[k, y_rows, :], ybuf.at[k, y_rows, :], yg_send.at[0], yg_recv.at[k], (row, q))
 
     def st_panel(k):
         if k in across_first:
             total = sbuf[k, 0]
         else:
-            remote(xrec.at[k], xrec.at[k], xs_send.at[k], xs_recv.at[k], (p, across)).wait_recv()
+            came(xrec.at[k], xs_recv.at[k])
             total = sbuf[k, far] + xrec[k]
         y = total * (-mask_of(k, p))
         ybuf[k, y_rows, :] = y
         for g in range(2):
             y_out[pl.ds(2 * k + g, ROWS, stride=12), :] = y[:, 128 * g : 128 * g + 128]
         near = p - core + k % 2
-        for n, turn in enumerate((2, 4, 12, 6, 14, 8, 10)):
+        for turn in (8, 10, 4, 12, 6, 14, 2):
             row = (near ^ (turn & 2)) + (turn & 12) & 15
-            go(y_copy(k, row, n + 1))
+            y_copy(k, row).start()
 
         @pl.when(core != k % 2)
         def _():
-            y_copy(k, other, 0).start()
+            y_copy(k, other).start()
 
     def st_spread_wait(k):
-        def one(i, carry):
-            t = (p + i) & 15
-            remote(e1r.at[t], e1r.at[t], e1_send.at[t], e1_recv.at[t], (other, q)).wait_recv()
-            return carry
-
-        lax.fori_loop(1, GRID, one, 0)
+        came(e1r.at[pl.ds(0, GRID - 1)], e1_recv.at[0])
 
     def e2_copy(n, w, t):
         column = 8 * core + t
         return remote(
-            e2s.at[n, w, t], e2r.at[n, q], e2_send.at[n, w, t], e2_recv.at[n, q], (pair + w, column)
+            e2s.at[n, w, t], e2r.at[n, q], e2_send.at[0], e2_recv.at[n], (pair + w, column)
         )
 
     def elsewhere(w, t):
@@ -418,14 +381,7 @@
         left = [split(jnp.concatenate([left[0][u], left[1][u]], axis=0)) for u in range(4)]
         unit = 2 * n + core
 
-        def one(i, carry):
-            row = (p + i) & 15
-            rows = pl.ds(pl.multiple_of(ROWS * row, ROWS), ROWS)
-            piece = ybuf.at[unit, rows, :]
-            remote(piece, piece, yg_send.at[n, 0], yg_recv.at[unit, row], (other, q)).wait_recv()
-            return carry
-
-        lax.fori_loop(1, GRID, one, 0)
+        came(ybuf.at[unit, pl.ds(0, ROWS * (GRID - 1)), :], yg_recv.at[unit])
         y = ybuf[unit].reshape(GRID, 4, 8, COLS)
         total = None
         for u in range(4):
@@ -457,22 +413,44 @@
             e2r[n, q] = e2s[n, core, q & 7]
 
     def st_result(n):
-        def one(i, carry):
-            t = (q + i) & 15
-
-            @pl.when(jnp.logical_or(t != q, far != core))
-            def _():
-                remote(e2r.at[n, t], e2r.at[n, t], e1_send.at[0], e2_recv.at[n, t], (other, q)).wait_recv()
-
-            return carry
-
-        lax.fori_loop(0, GRID, one, 0)
+        @pl.when(far == core)
+        def _():
+            came(e2r.at[n, pl.ds(0, GRID - 1)], e2_recv.at[n])
+
+        @pl.when(far != core)
+        def _():
+            came(e2r.at[n], e2_recv.at[n])
+
         total = jnp.sum(e2r[n], axis=0)
         parts = [total] + [pltpu.roll(total, 128 - 32 * u, 1) for u in range(1, 4)]
         square = jnp.concatenate(parts, axis=0)
         d_out[n] = piv_in[n] - square[:, :ROWS]
 
+    def st_drain(n):
+        if n == 0:
+
+            @pl.when(jnp.logical_not(keeps))
+            def _():
+                went(src, a_send.at[0])
+
+            @pl.when(jnp.logical_not(stays))
+            def _():
+                went(taken, land_send.at[0])
+
+            went(xbuf.at[:, pl.ds(0, 15 * ROWS), :], xg_send.at[0])
+            went(e1r.at[pl.ds(0, GRID - 1)], e1_send.at[0])
+            return
+        for k in range(UNITS):
+            if k in across_first:
+                half_copy(k).wait_send()
+                went(rbuf.at[k, 0], rs_send.at[k])
+            else:
+                went(xrec.at[k], xs_send.at[k])
+                went(rbuf.at[k], rs_send.at[k])
+        went(ybuf.at[:, pl.ds(0, 240), :], yg_send.at[0])
+
     stages = {
+        "drain": st_drain,
         "take": st_take,
         "prepare": st_prepare,
         "own": st_own,
@@ -492,40 +470,13 @@
         with jax.named_scope(f"{name}_{k}"):
             stages[name](k)
 
-    for k in range(UNITS):
-
-        @pl.when(jnp.logical_not(keeps))
-        def _():
-            take_copy(k).wait_send()
-
-        @pl.when(jnp.logical_not(stays))
-        def _():
-            land_copy(k, 0).wait_send()
-
-        @pl.when(core != k % 2)
-        def _():
-            y_copy(k, other, 0).wait_send()
-
-    for n in range(NSUP):
-
-        def two(t, carry, n=n):
-            for w in range(2):
-
-                @pl.when(elsewhere(w, t))
-                def _():
-                    e2_copy(n, w, t).wait_send()
-
-            return carry
-
-        lax.fori_loop(0, 8, two, 0)
-
-    def one(i, carry):
-        spread_copy((p + i) & 15).wait_send()
-        return carry
-
-    lax.fori_loop(1, GRID, one, 0)
-    for copy in sends:
-        copy.wait_send()
+    @pl.when(far == core)
+    def _():
+        went(e2r.at[:, pl.ds(0, GRID - 1)], e2_send.at[0])
+
+    @pl.when(far != core)
+    def _():
+        went(e2r, e2_send.at[0])
 
 
 def body(ancestor_inverse, factor_panel, pivot_inverse, structure):
@@ -550,30 +501,31 @@
             pltpu.VMEM((UNITS, ROWS, COLS), F32),
             pltpu.VMEM((UNITS, WIDTH, COLS), F32),
             pltpu.VMEM((UNITS, WIDTH, COLS), F32),
-            pltpu.VMEM((UNITS, 2, 2, 4, ROWS, COLS), F32),
+            pltpu.VMEM((UNITS, 2, 7, ROWS, COLS), F32),
             pltpu.VMEM((UNITS, 2, ROWS, COLS), F32),
             pltpu.VMEM((UNITS, ROWS, COLS), F32),
-            pltpu.VMEM((len(FIRST_ACROSS), 256, COLS), F32),
+            pltpu.VMEM((1, 256, COLS), F32),
             pltpu.VMEM((UNITS, WIDTH, COLS), F32),
             pltpu.VMEM((GRID, NSUP * 8, 128), F32),
             pltpu.VMEM((GRID, 2, NSUP * 8, 128), F32),
             pltpu.VMEM((NSUP, 2, 8, 8, 128), F32),
             pltpu.VMEM((NSUP, GRID, 8, 128), F32),
             dma((4,)),
+            dma((1,)),
+            dma((UNITS,)),
+            dma((1,)),
+            dma((1,)),
+            dma((UNITS, 5)),
+            dma((UNITS,)),
+            dma((UNITS, 2, 4)),
             dma((UNITS,)),
             dma((UNITS,)),
-            dma((UNITS, 16)),
-            dma((UNITS, 16)),
-            dma((UNITS, 2, 2, 4)),
-            dma((UNITS, 2, 2, 4)),
+            dma((1,)),
             dma((UNITS,)),
-            dma((UNITS,)),
-            dma((UNITS, 8)),
-            dma((UNITS, GRID)),
-            dma((GRID,)),
-            dma((GRID,)),
-            dma((NSUP, 2, 8)),
-            dma((NSUP, GRID)),
+            dma((1,)),
+            dma((1,)),
+            dma((1,)),
+            dma((NSUP,)),
         ],
         compiler_params=pltpu.CompilerParams(
             collective_id=0, has_side_effects=True, vmem_limit_bytes=VMEM_LIMIT

time: 91.1 us -> 84.1 us (0.923)
  Pallas kernels: 89 us -> 81.4 us
    pallas_call x1, Pallas kernels: 89 us -> 81.4 us  [body(): pl.pallas_call(kernel, out_shape=(pltpu.VMEM((ROWS * NSUP * 4, 128), F32)...]
where the time goes in v4:
time: 84.1 us; the launch traced here: 83.3 us
  Pallas kernels  81.4 us (97%)
  local copies, waits for them, and re-layouts  1.3 us (2%)
    pallas_call x1, Pallas kernels, body(): pl.pallas_call(kernel, out_shape=(pltpu.VMEM((ROWS * NSUP * 4, 128), F32)...  81.4 us

profile of v4, /device:TPU:7, one launch (start us, length us, event | category | flops | bytes accessed | tf_op | source)
XLA Modules:
  0.0 83.3 jit_solution(18200726431839403615)
XLA Ops:
  0.6 81.4 %level.1 = (f32[384,128]{1,0:T(8,128)S(1)}, f32[3,32,32]{2,1,0:T(8,128)S(1)}) custom-call(f32[512,512]{1,0:T(8,128)} %bitcast.5, f32[384,128]{1,0:T(8,128)} %bitcast.6, f32[3,32,32]{2,1,0:T(8,128)} %piv_hbm.1, s32[3,16]{1,0:T(4,128)} %bitcast.7), custom_call_target="tpu_custom_call" | custom-call | tf_op jit(solution)/shard_map/level/pallas_call | solution.py:485
  82.0 0.7 copy.10
  82.7 0.6 copy.11

commit v5 on v4

--- a/solution.py
+++ b/solution.py
@@ -15,7 +15,7 @@
 UNITS = 6
 COLS = 256
 IN_FLIGHT = 3
-FIRST_ACROSS = ()
+FIRST_ACROSS = (1, 4)
 
 
 VMEM_LIMIT = 40 * 1024 * 1024
@@ -25,14 +25,14 @@
     ("take", 0), ("prepare", 0), ("take", 1), ("take", 2), ("take", 3), ("take", 4), ("take", 5), ("own", 0),
     ("second", 0), ("own", 1), ("second", 1), ("own", 2), ("second", 2), ("own", 3), ("second", 3),
     ("forward", 0), ("own", 4), ("second", 4), ("product", 0), ("own", 5), ("launch", 0), ("second", 5),
-    ("forward", 1), ("product", 1), ("launch", 1), ("forward", 2), ("sum0", 0), ("product", 2), ("launch", 2),
-    ("forward", 3), ("sum0", 1), ("sum1", 0), ("product", 3), ("launch", 3), ("forward", 4), ("sum0", 2),
-    ("sum1", 1), ("product", 4), ("forward", 5), ("sum2", 0), ("sum0", 3), ("product", 5), ("spread", 0),
-    ("sum1", 2), ("sum2", 1), ("sum3", 0), ("launch", 4), ("sum1", 3), ("sum2", 2), ("sum3", 1),
-    ("launch", 5), ("panel", 0), ("sum0", 4), ("sum2", 3), ("sum3", 2), ("panel", 1), ("sum0", 5),
-    ("sum1", 4), ("sum3", 3), ("panel", 2), ("sum1", 5), ("sum2", 4), ("panel", 3), ("arrived", 0),
-    ("diagonal", 0), ("sum3", 4), ("sum2", 5), ("sum3", 5), ("panel", 4), ("diagonal", 1), ("panel", 5),
-    ("drain", 0), ("diagonal", 2), ("drain", 1), ("result", 0), ("result", 1), ("result", 2),
+    ("forward", 1), ("product", 1), ("forward", 2), ("sum0", 0), ("product", 2), ("launch", 2),
+    ("forward", 3), ("sum1", 0), ("product", 3), ("launch", 3), ("forward", 4), ("sum0", 2), ("sum2", 0),
+    ("product", 4), ("forward", 5), ("sum0", 3), ("launch", 1), ("sum1", 2), ("product", 5), ("sum3", 0),
+    ("launch", 5), ("spread", 0), ("sum1", 3), ("sum0", 1), ("sum2", 2), ("sum0", 5), ("sum2", 3),
+    ("sum1", 1), ("panel", 0), ("sum3", 2), ("launch", 4), ("sum1", 5), ("sum3", 3), ("sum2", 1), ("sum0", 4),
+    ("sum2", 5), ("sum3", 1), ("panel", 1), ("sum1", 4), ("sum3", 5), ("sum2", 4), ("panel", 2), ("panel", 3),
+    ("sum3", 4), ("panel", 4), ("arrived", 0), ("diagonal", 0), ("panel", 5), ("drain", 0), ("diagonal", 1),
+    ("diagonal", 2), ("drain", 1), ("result", 0), ("result", 1), ("result", 2),
 )
 
 
@@ -79,7 +79,7 @@
 def kernel(
     a_hbm, l_hbm, piv_hbm, s_hbm,
     y_out, d_out,
-    a_in, l_in, piv_in, s_in, a_high, a_low, src, taken, xbuf, pbuf, rbuf, sbuf, xrec, xhalf, ybuf,
+    a_in, l_in, piv_in, s_in, a_high, a_low, src, taken, xbuf, pbuf, rbuf, sbuf, xrec, xhalf, ystage, yq, l_high, l_low,
     e1s, e1r, e2s, e2r,
     load_sem, a_send, a_recv, land_send, xg_send, xg_recv, rs_send, rs_recv, xs_send, xs_recv, yg_send, yg_recv,
     e1_send, e1_recv, e2_send, e2_recv,
@@ -222,13 +222,8 @@
         loads[1].wait()
         a_high[...], a_low[...] = split(a_in[...])
         for n in range(NSUP):
-
-            for h in range(2):
-
-                def put(t, tile, n=n, h=h):
-                    e1s[8 * h + t, 8 * n : 8 * n + 8, :] = tile
-
-                pack(src[2 * n + h], put)
+            for g in range(4):
+                e1s[g, n] = src[2 * n + g // 2, :, 128 * (g % 2) : 128 * (g % 2) + 128]
         loads[2].wait()
         loads[3].wait()
 
@@ -323,11 +318,11 @@
                 start(remote(sbuf.at[k, 1 - far], xrec.at[k], xs_send.at[k], xs_recv.at[k], (p, across)))
 
     core = p & 1
-    pair = p - core
+    side = (p >> 1) & 1
+    mine = p & 3
 
     def spread_copy(t):
-        tiles = pl.ds(2 * (t >> 1), 2)
-        return remote(e1s.at[tiles], e1r.at[p], e1_send.at[0], e1_recv.at[0], (t, q))
+        return remote(e1s.at[t >> 2], e1r.at[p], e1_send.at[0], e1_recv.at[0], (t, q))
 
     def st_spread(k):
         def one(i, carry):
@@ -335,12 +330,14 @@
             return carry
 
         lax.fori_loop(1, GRID, one, 0)
-        e1r[p] = e1s[pl.ds(pair, 2)]
+        e1r[p] = e1s[p >> 2]
 
     y_rows = pl.ds(pl.multiple_of(ROWS * p, ROWS), ROWS)
 
-    def y_copy(k, row):
-        return remote(ybuf.at[k, y_rows, :], ybuf.at[k, y_rows, :], yg_send.at[0], yg_recv.at[k], (row, q))
+    def y_copy(k, row, c):
+        return remote(
+            ystage.at[k, :, pl.ds(128 * c, 128)], yq.at[k // 2, y_rows, :], yg_send.at[0], yg_recv.at[k // 2], (row, q)
+        )
 
     def st_panel(k):
         if k in across_first:
@@ -349,75 +346,63 @@
             came(xrec.at[k], xs_recv.at[k])
             total = sbuf[k, far] + xrec[k]
         y = total * (-mask_of(k, p))
-        ybuf[k, y_rows, :] = y
+        ystage[k] = y
         for g in range(2):
             y_out[pl.ds(2 * k + g, ROWS, stride=12), :] = y[:, 128 * g : 128 * g + 128]
-        near = p - core + k % 2
-        for turn in (8, 10, 4, 12, 6, 14, 2):
-            row = (near ^ (turn & 2)) + (turn & 12) & 15
-            y_copy(k, row).start()
-
-        @pl.when(core != k % 2)
-        def _():
-            y_copy(k, other).start()
+        for up in (8, 4, 12, 0):
+            for c in range(2):
+                row = 4 * (((p + up) & 15) >> 2) + 2 * (k % 2) + c
+                if up:
+                    y_copy(k, row, c).start()
+                else:
+
+                    @pl.when(mine != 2 * (k % 2) + c)
+                    def _():
+                        y_copy(k, row, c).start()
+
+                    @pl.when(mine == 2 * (k % 2) + c)
+                    def _():
+                        yq[k // 2, y_rows, :] = y[:, 128 * c : 128 * c + 128]
 
     def st_spread_wait(k):
         came(e1r.at[pl.ds(0, GRID - 1)], e1_recv.at[0])
+        for n in range(NSUP):
+            l_high[n], l_low[n] = split(e1r[:, n].reshape(WIDTH, 128).T)
+
+    same = mine == (q >> 2)
 
     def e2_copy(n, w, t):
-        column = 8 * core + t
         return remote(
-            e2s.at[n, w, t], e2r.at[n, q], e2_send.at[0], e2_recv.at[n], (pair + w, column)
+            e2s.at[n, w, t], e2r.at[n, q], e2_send.at[0], e2_recv.at[n], (p - mine + w, 4 * mine + t)
         )
 
-    def elsewhere(w, t):
-        return jnp.logical_or(pair + w != p, 8 * core + t != q)
-
     def st_diagonal(n):
-        left = []
-        for w in range(2):
-            turned = e1r[:, w, 8 * n : 8 * n + 8, :].reshape(128, 128).T
-            left.append([turned[32 * u : 32 * u + 32, :] for u in range(4)])
-        left = [split(jnp.concatenate([left[0][u], left[1][u]], axis=0)) for u in range(4)]
-        unit = 2 * n + core
-
-        came(ybuf.at[unit, pl.ds(0, ROWS * (GRID - 1)), :], yg_recv.at[unit])
-        y = ybuf[unit].reshape(GRID, 4, 8, COLS)
-        total = None
-        for u in range(4):
-            l_high, l_low = left[u]
-            y_high, y_low = split(y[:, u].reshape(128, COLS))
-            term = dot(l_high, y_high) + dot(l_high, y_low) + dot(l_low, y_high)
-            total = term if total is None else total + term
-        for w in range(2):
+        came(yq.at[n, pl.ds(0, ROWS * (GRID - 1)), :], yg_recv.at[n])
+        y_high, y_low = split(yq[n])
+        total = dot(l_high[n], y_high) + dot(l_high[n], y_low) + dot(l_low[n], y_high)
+        for w in range(4):
 
             def put(t, tile, w=w):
                 e2s[n, w, t] = tile
 
             pack(total[32 * w : 32 * w + 32, :], put)
-
-        def two(i, carry):
-            t = (q + i) & 7
-            for w in range(2):
-
-                @pl.when(elsewhere(w, t))
+        for w in range(4):
+            for t in range(4):
+
+                @pl.when(jnp.logical_or(mine != w, 4 * mine + t != q))
                 def _():
                     e2_copy(n, w, t).start()
 
-            return carry
-
-        lax.fori_loop(0, 8, two, 0)
-
-        @pl.when(far == core)
-        def _():
-            e2r[n, q] = e2s[n, core, q & 7]
+        @pl.when(same)
+        def _():
+            e2r[n, q] = e2s[n, mine, q & 3]
 
     def st_result(n):
-        @pl.when(far == core)
+        @pl.when(same)
         def _():
             came(e2r.at[n, pl.ds(0, GRID - 1)], e2_recv.at[n])
 
-        @pl.when(far != core)
+        @pl.when(jnp.logical_not(same))
         def _():
             came(e2r.at[n], e2_recv.at[n])
 
@@ -447,7 +432,7 @@
             else:
                 went(xrec.at[k], xs_send.at[k])
                 went(rbuf.at[k], rs_send.at[k])
-        went(ybuf.at[:, pl.ds(0, 240), :], yg_send.at[0])
+        went(yq.at[:, pl.ds(0, ROWS * (GRID - 1)), :], yg_send.at[0])
 
     stages = {
         "drain": st_drain,
@@ -470,11 +455,11 @@
         with jax.named_scope(f"{name}_{k}"):
             stages[name](k)
 
-    @pl.when(far == core)
+    @pl.when(same)
     def _():
         went(e2r.at[:, pl.ds(0, GRID - 1)], e2_send.at[0])
 
-    @pl.when(far != core)
+    @pl.when(jnp.logical_not(same))
     def _():
         went(e2r, e2_send.at[0])
 
@@ -504,11 +489,14 @@
             pltpu.VMEM((UNITS, 2, 7, ROWS, COLS), F32),
             pltpu.VMEM((UNITS, 2, ROWS, COLS), F32),
             pltpu.VMEM((UNITS, ROWS, COLS), F32),
-            pltpu.VMEM((1, 256, COLS), F32),
-            pltpu.VMEM((UNITS, WIDTH, COLS), F32),
-            pltpu.VMEM((GRID, NSUP * 8, 128), F32),
-            pltpu.VMEM((GRID, 2, NSUP * 8, 128), F32),
-            pltpu.VMEM((NSUP, 2, 8, 8, 128), F32),
+            pltpu.VMEM((len(FIRST_ACROSS), 256, COLS), F32),
+            pltpu.VMEM((UNITS, ROWS, COLS), F32),
+            pltpu.VMEM((NSUP, WIDTH, 128), F32),
+            pltpu.VMEM((NSUP, 128, WIDTH), BF16),
+            pltpu.VMEM((NSUP, 128, WIDTH), BF16),
+            pltpu.VMEM((4, NSUP, ROWS, 128), F32),
+            pltpu.VMEM((GRID, NSUP, ROWS, 128), F32),
+            pltpu.VMEM((NSUP, 4, 4, 8, 128), F32),
             pltpu.VMEM((NSUP, GRID, 8, 128), F32),
             dma((4,)),
             dma((1,)),
@@ -521,7 +509,7 @@
             dma((UNITS,)),
             dma((UNITS,)),
             dma((1,)),
-            dma((UNITS,)),
+            dma((NSUP,)),
             dma((1,)),
             dma((1,)),
             dma((1,)),

time: 84.1 us -> 80.8 us (0.961)
  Pallas kernels: 81.4 us -> 77.5 us
    pallas_call x1, Pallas kernels: 81.4 us -> 77.5 us  [body(): pl.pallas_call(kernel, out_shape=(pltpu.VMEM((ROWS * NSUP * 4, 128), F32)...]
where the time goes in v5:
time: 80.8 us; the launch traced here: 79.5 us
  Pallas kernels  77.5 us (96%)
  local copies, waits for them, and re-layouts  1.3 us (2%)
    pallas_call x1, Pallas kernels, body(): pl.pallas_call(kernel, out_shape=(pltpu.VMEM((ROWS * NSUP * 4, 128), F32)...  77.5 us

profile of v5, /device:TPU:7, one launch (start us, length us, event | category | flops | bytes accessed | tf_op | source)
XLA Modules:
  0.0 79.5 jit_solution(8451099759233068727)
XLA Ops:
  0.6 77.5 %level.1 = (f32[384,128]{1,0:T(8,128)S(1)}, f32[3,32,32]{2,1,0:T(8,128)S(1)}) custom-call(f32[512,512]{1,0:T(8,128)} %bitcast.5, f32[384,128]{1,0:T(8,128)} %bitcast.6, f32[3,32,32]{2,1,0:T(8,128)} %piv_hbm.1, s32[3,16]{1,0:T(4,128)} %bitcast.7), custom_call_target="tpu_custom_call" | custom-call | tf_op jit(solution)/shard_map/level/pallas_call | solution.py:470
  78.2 0.7 copy.10
  78.8 0.6 copy.11

commit v6 on v5

--- a/solution.py
+++ b/solution.py
@@ -12,27 +12,36 @@
 NSUP = 3
 WIDTH = 512
 GRID = 16
-UNITS = 6
-COLS = 256
+UNITS = 12
+COLS = 128
 IN_FLIGHT = 3
-FIRST_ACROSS = (1, 4)
+FIRST_ACROSS = (2, 4, 7, 9)
 
 
 VMEM_LIMIT = 40 * 1024 * 1024
 
 
 ORDER = (
-    ("take", 0), ("prepare", 0), ("take", 1), ("take", 2), ("take", 3), ("take", 4), ("take", 5), ("own", 0),
-    ("second", 0), ("own", 1), ("second", 1), ("own", 2), ("second", 2), ("own", 3), ("second", 3),
-    ("forward", 0), ("own", 4), ("second", 4), ("product", 0), ("own", 5), ("launch", 0), ("second", 5),
-    ("forward", 1), ("product", 1), ("forward", 2), ("sum0", 0), ("product", 2), ("launch", 2),
-    ("forward", 3), ("sum1", 0), ("product", 3), ("launch", 3), ("forward", 4), ("sum0", 2), ("sum2", 0),
-    ("product", 4), ("forward", 5), ("sum0", 3), ("launch", 1), ("sum1", 2), ("product", 5), ("sum3", 0),
-    ("launch", 5), ("spread", 0), ("sum1", 3), ("sum0", 1), ("sum2", 2), ("sum0", 5), ("sum2", 3),
-    ("sum1", 1), ("panel", 0), ("sum3", 2), ("launch", 4), ("sum1", 5), ("sum3", 3), ("sum2", 1), ("sum0", 4),
-    ("sum2", 5), ("sum3", 1), ("panel", 1), ("sum1", 4), ("sum3", 5), ("sum2", 4), ("panel", 2), ("panel", 3),
-    ("sum3", 4), ("panel", 4), ("arrived", 0), ("diagonal", 0), ("panel", 5), ("drain", 0), ("diagonal", 1),
-    ("diagonal", 2), ("drain", 1), ("result", 0), ("result", 1), ("result", 2),
+    ("take", 0), ("prepare", 0), ("take", 1), ("take", 2), ("take", 3), ("take", 4), ("take", 5), ("take", 6),
+    ("take", 7), ("take", 8), ("take", 9), ("take", 10), ("take", 11), ("own", 0), ("second", 0), ("own", 1),
+    ("second", 1), ("own", 2), ("second", 2), ("own", 3), ("second", 3), ("own", 4), ("second", 4),
+    ("own", 5), ("forward", 0), ("second", 5), ("own", 6), ("second", 6), ("own", 7), ("forward", 1),
+    ("product", 0), ("second", 7), ("own", 8), ("launch", 0), ("second", 8), ("own", 9), ("forward", 2),
+    ("product", 1), ("second", 9), ("own", 10), ("launch", 1), ("second", 10), ("own", 11), ("forward", 3),
+    ("product", 2), ("sum0", 0), ("second", 11), ("forward", 4), ("product", 3), ("sum0", 1), ("launch", 3),
+    ("forward", 5), ("product", 4), ("sum1", 0), ("forward", 6), ("product", 5), ("sum1", 1), ("launch", 5),
+    ("sum0", 3), ("forward", 7), ("product", 6), ("sum2", 0), ("launch", 6), ("launch", 2), ("forward", 8),
+    ("product", 7), ("sum2", 1), ("sum0", 5), ("forward", 9), ("product", 8), ("sum1", 3), ("launch", 8),
+    ("launch", 4), ("sum3", 0), ("forward", 10), ("sum0", 6), ("product", 9), ("sum0", 2), ("sum3", 1),
+    ("forward", 11), ("sum1", 5), ("product", 10), ("launch", 10), ("sum2", 3), ("sum0", 8), ("product", 11),
+    ("sum0", 4), ("launch", 11), ("spread", 0), ("panel", 0), ("sum1", 6), ("sum1", 2), ("sum2", 5),
+    ("sum0", 10), ("sum3", 3), ("launch", 7), ("sum1", 8), ("panel", 1), ("sum1", 4), ("sum0", 11),
+    ("sum2", 6), ("sum2", 2), ("sum3", 5), ("launch", 9), ("sum1", 10), ("sum0", 7), ("sum2", 8), ("sum2", 4),
+    ("sum1", 11), ("sum3", 6), ("sum3", 2), ("panel", 2), ("sum0", 9), ("sum2", 10), ("sum1", 7), ("sum3", 8),
+    ("sum3", 4), ("panel", 4), ("sum2", 11), ("sum1", 9), ("sum3", 10), ("panel", 3), ("sum2", 7),
+    ("panel", 5), ("sum3", 11), ("panel", 6), ("sum2", 9), ("sum3", 7), ("panel", 8), ("panel", 7),
+    ("panel", 10), ("sum3", 9), ("panel", 9), ("arrived", 0), ("diagonal", 0), ("panel", 11), ("drain", 0),
+    ("diagonal", 1), ("diagonal", 2), ("drain", 1), ("result", 0), ("result", 1), ("result", 2),
 )
 
 
@@ -138,8 +147,7 @@
 
     loads[0].wait()
     for u in range(UNITS):
-        for g in range(2):
-            src[u, :, 128 * g : 128 * g + 128] = l_in[pl.ds(2 * u + g, ROWS, stride=12), :]
+        src[u] = l_in[pl.ds(u, ROWS, stride=12), :]
     with jax.named_scope("barrier"):
         pl.semaphore_wait(
             barrier, jnp.where(keeps, 10, 11) + jnp.where(stays, 0, 1) + jnp.where(origin == q, 0, 1)
@@ -175,9 +183,9 @@
         return xbuf.at[k, pl.ds(0, ROWS * count), :]
 
     def push_all(k, kind):
+        push(k, kind, 6 + kind, opposite)
         push(k, kind, 2 + kind, above)
         push(k, kind, 4 + kind, below)
-        push(k, kind, 6 + kind, opposite)
         push(k, kind, 8 + kind, other)
 
     def take_copy(k):
@@ -223,7 +231,7 @@
         a_high[...], a_low[...] = split(a_in[...])
         for n in range(NSUP):
             for g in range(4):
-                e1s[g, n] = src[2 * n + g // 2, :, 128 * (g % 2) : 128 * (g % 2) + 128]
+                e1s[g, n] = src[4 * n + g]
         loads[2].wait()
         loads[3].wait()
 
@@ -275,7 +283,7 @@
         )
 
     def mask_of(k, index):
-        return s_in[k // 2, index].astype(F32)
+        return s_in[k // 4, index].astype(F32)
 
     def half_copy(k):
         rows = pl.ds(pl.multiple_of(256 * (1 - far), 256), 256)
@@ -334,10 +342,8 @@
 
     y_rows = pl.ds(pl.multiple_of(ROWS * p, ROWS), ROWS)
 
-    def y_copy(k, row, c):
-        return remote(
-            ystage.at[k, :, pl.ds(128 * c, 128)], yq.at[k // 2, y_rows, :], yg_send.at[0], yg_recv.at[k // 2], (row, q)
-        )
+    def y_copy(k, row):
+        return remote(ystage.at[k], yq.at[k // 4, y_rows, :], yg_send.at[0], yg_recv.at[k // 4], (row, q))
 
     def st_panel(k):
         if k in across_first:
@@ -347,22 +353,20 @@
             total = sbuf[k, far] + xrec[k]
         y = total * (-mask_of(k, p))
         ystage[k] = y
-        for g in range(2):
-            y_out[pl.ds(2 * k + g, ROWS, stride=12), :] = y[:, 128 * g : 128 * g + 128]
+        y_out[pl.ds(k, ROWS, stride=12), :] = y
         for up in (8, 4, 12, 0):
-            for c in range(2):
-                row = 4 * (((p + up) & 15) >> 2) + 2 * (k % 2) + c
-                if up:
-                    y_copy(k, row, c).start()
-                else:
-
-                    @pl.when(mine != 2 * (k % 2) + c)
-                    def _():
-                        y_copy(k, row, c).start()
-
-                    @pl.when(mine == 2 * (k % 2) + c)
-                    def _():
-                        yq[k // 2, y_rows, :] = y[:, 128 * c : 128 * c + 128]
+            row = 4 * (((p + up) & 15) >> 2) + k % 4
+            if up:
+                y_copy(k, row).start()
+            else:
+
+                @pl.when(mine != k % 4)
+                def _():
+                    y_copy(k, row).start()
+
+                @pl.when(mine == k % 4)
+                def _():
+                    yq[k // 4, y_rows, :] = y
 
     def st_spread_wait(k):
         came(e1r.at[pl.ds(0, GRID - 1)], e1_recv.at[0])

time: 80.8 us -> 78.1 us (0.967); the launches traced: 79.5 us -> 78 us
  Pallas kernels: 77.5 us -> 76.1 us
    pallas_call x1, Pallas kernels: 77.5 us -> 76.1 us  [body(): pl.pallas_call(kernel, out_shape=(pltpu.VMEM((ROWS * NSUP * 4, 128), F32)...]
where the time goes in v6:
time: 78.1 us; the launch traced here: 78 us
  Pallas kernels  76.1 us (97%)
  local copies, waits for them, and re-layouts  1.3 us (2%)
    pallas_call x1, Pallas kernels, body(): pl.pallas_call(kernel, out_shape=(pltpu.VMEM((ROWS * NSUP * 4, 128), F32)...  76.1 us

profile of v6, /device:TPU:7, one launch (start us, length us, event | category | flops | bytes accessed | tf_op | source)
XLA Modules:
  0.0 78.0 jit_solution(7580177976961880210)
XLA Ops:
  0.6 76.1 %level.1 = (f32[384,128]{1,0:T(8,128)S(1)}, f32[3,32,32]{2,1,0:T(8,128)S(1)}) custom-call(f32[512,512]{1,0:T(8,128)} %bitcast.5, f32[384,128]{1,0:T(8,128)} %bitcast.6, f32[3,32,32]{2,1,0:T(8,128)} %piv_hbm.1, s32[3,16]{1,0:T(4,128)} %bitcast.7), custom_call_target="tpu_custom_call" | custom-call | tf_op jit(solution)/shard_map/level/pallas_call | solution.py:474
  76.7 0.7 copy.10
  77.4 0.6 copy.11

commit v7 on v6

--- a/solution.py
+++ b/solution.py
@@ -257,6 +257,8 @@
     across_first = FIRST_ACROSS
     halves = [(0,) if k in across_first else (0, 1) for k in range(UNITS)]
 
+    flows = [(k, h) for k in range(UNITS) for h in halves[k]]
+
     def steps(k, h, way):
         return 4 if (k + h + way) % 2 == 0 else 3
 
@@ -276,8 +278,8 @@
             remote(
                 pbuf.at[k, block_rows(k, h, sent_block(k, h, way, t)), :],
                 rbuf.at[k, h, slot(t, way)],
-                rs_send.at[k],
-                rs_recv.at[k, h, t],
+                rs_send.at[0],
+                rs_recv.at[flows.index((k, h)), t],
                 (p, z_down if way == 0 else z_up),
             )
         )
@@ -288,7 +290,7 @@
     def half_copy(k):
         rows = pl.ds(pl.multiple_of(256 * (1 - far), 256), 256)
         at = across_first.index(k)
-        return remote(pbuf.at[k, rows, :], xhalf.at[at], xs_send.at[k], xs_recv.at[k], (p, across))
+        return remote(pbuf.at[k, rows, :], xhalf.at[at], xs_send.at[0], xs_recv.at[k], (p, across))
 
     def st_product(k):
         came(pieces(k, 8), xg_recv.at[k, 4])
@@ -310,7 +312,7 @@
 
     def st_sum(k, t):
         for h in halves[k]:
-            came(rbuf.at[k, h, pl.ds(2 * t, 2 if t < 3 else 1)], rs_recv.at[k, h, t])
+            came(rbuf.at[k, h, pl.ds(2 * t, 2 if t < 3 else 1)], rs_recv.at[flows.index((k, h)), t])
             for way in range(2):
                 if t < steps(k, h, way) - 1:
                     rows = block_rows(k, h, sent_block(k, h, way, t + 1))
@@ -323,7 +325,7 @@
                     total = total + rbuf[k, h, slot(steps(k, h, way) - 1, way)]
                 sbuf[k, h] = total
             if k not in across_first:
-                start(remote(sbuf.at[k, 1 - far], xrec.at[k], xs_send.at[k], xs_recv.at[k], (p, across)))
+                start(remote(sbuf.at[k, 1 - far], xrec.at[k], xs_send.at[0], xs_recv.at[k], (p, across)))
 
     core = p & 1
     side = (p >> 1) & 1
@@ -429,13 +431,8 @@
             went(xbuf.at[:, pl.ds(0, 15 * ROWS), :], xg_send.at[0])
             went(e1r.at[pl.ds(0, GRID - 1)], e1_send.at[0])
             return
-        for k in range(UNITS):
-            if k in across_first:
-                half_copy(k).wait_send()
-                went(rbuf.at[k, 0], rs_send.at[k])
-            else:
-                went(xrec.at[k], xs_send.at[k])
-                went(rbuf.at[k], rs_send.at[k])
+        went(xbuf.at[pl.ds(0, 5), pl.ds(0, 256), :], xs_send.at[0])
+        went(rbuf.at[pl.ds(0, UNITS - len(across_first) // 2)], rs_send.at[0])
         went(yq.at[:, pl.ds(0, ROWS * (GRID - 1)), :], yg_send.at[0])
 
     stages = {
@@ -508,9 +505,9 @@
             dma((1,)),
             dma((1,)),
             dma((UNITS, 5)),
-            dma((UNITS,)),
-            dma((UNITS, 2, 4)),
-            dma((UNITS,)),
+            dma((1,)),
+            dma((2 * UNITS - len(FIRST_ACROSS), 4)),
+            dma((1,)),
             dma((UNITS,)),
             dma((1,)),
             dma((NSUP,)),

time: 78.1 us -> 77.8 us (level)
  no operation moved by 1% of the time
where the time goes in v7:
time: 77.8 us; the launch traced here: 77.7 us
  Pallas kernels  75.7 us (97%)
  local copies, waits for them, and re-layouts  1.3 us (2%)
    pallas_call x1, Pallas kernels, body(): pl.pallas_call(kernel, out_shape=(pltpu.VMEM((ROWS * NSUP * 4, 128), F32)...  75.7 us

profile of v7, /device:TPU:7, one launch (start us, length us, event | category | flops | bytes accessed | tf_op | source)
XLA Modules:
  0.0 77.7 jit_solution(9587228037367905681)
XLA Ops:
  0.6 75.7 %level.1 = (f32[384,128]{1,0:T(8,128)S(1)}, f32[3,32,32]{2,1,0:T(8,128)S(1)}) custom-call(f32[512,512]{1,0:T(8,128)} %bitcast.5, f32[384,128]{1,0:T(8,128)} %bitcast.6, f32[3,32,32]{2,1,0:T(8,128)} %piv_hbm.1, s32[3,16]{1,0:T(4,128)} %bitcast.7), custom_call_target="tpu_custom_call" | custom-call | tf_op jit(solution)/shard_map/level/pallas_call | solution.py:471
  76.4 0.7 copy.10
  77.0 0.6 copy.11

commit v8 on v7

--- a/solution.py
+++ b/solution.py
@@ -30,18 +30,18 @@
     ("product", 1), ("second", 9), ("own", 10), ("launch", 1), ("second", 10), ("own", 11), ("forward", 3),
     ("product", 2), ("sum0", 0), ("second", 11), ("forward", 4), ("product", 3), ("sum0", 1), ("launch", 3),
     ("forward", 5), ("product", 4), ("sum1", 0), ("forward", 6), ("product", 5), ("sum1", 1), ("launch", 5),
-    ("sum0", 3), ("forward", 7), ("product", 6), ("sum2", 0), ("launch", 6), ("launch", 2), ("forward", 8),
-    ("product", 7), ("sum2", 1), ("sum0", 5), ("forward", 9), ("product", 8), ("sum1", 3), ("launch", 8),
-    ("launch", 4), ("sum3", 0), ("forward", 10), ("sum0", 6), ("product", 9), ("sum0", 2), ("sum3", 1),
-    ("forward", 11), ("sum1", 5), ("product", 10), ("launch", 10), ("sum2", 3), ("sum0", 8), ("product", 11),
-    ("sum0", 4), ("launch", 11), ("spread", 0), ("panel", 0), ("sum1", 6), ("sum1", 2), ("sum2", 5),
-    ("sum0", 10), ("sum3", 3), ("launch", 7), ("sum1", 8), ("panel", 1), ("sum1", 4), ("sum0", 11),
-    ("sum2", 6), ("sum2", 2), ("sum3", 5), ("launch", 9), ("sum1", 10), ("sum0", 7), ("sum2", 8), ("sum2", 4),
-    ("sum1", 11), ("sum3", 6), ("sum3", 2), ("panel", 2), ("sum0", 9), ("sum2", 10), ("sum1", 7), ("sum3", 8),
-    ("sum3", 4), ("panel", 4), ("sum2", 11), ("sum1", 9), ("sum3", 10), ("panel", 3), ("sum2", 7),
-    ("panel", 5), ("sum3", 11), ("panel", 6), ("sum2", 9), ("sum3", 7), ("panel", 8), ("panel", 7),
-    ("panel", 10), ("sum3", 9), ("panel", 9), ("arrived", 0), ("diagonal", 0), ("panel", 11), ("drain", 0),
-    ("diagonal", 1), ("diagonal", 2), ("drain", 1), ("result", 0), ("result", 1), ("result", 2),
+    ("sum0", 3), ("forward", 7), ("product", 6), ("sum2", 0), ("launch", 2), ("launch", 6), ("forward", 8),
+    ("product", 7), ("sum2", 1), ("sum0", 5), ("forward", 9), ("product", 8), ("sum1", 3), ("launch", 4),
+    ("launch", 8), ("sum3", 0), ("sum0", 2), ("forward", 10), ("product", 9), ("sum0", 6), ("spread", 0),
+    ("sum3", 1), ("forward", 11), ("sum1", 5), ("product", 10), ("launch", 10), ("sum2", 3), ("sum0", 4),
+    ("product", 11), ("sum0", 8), ("launch", 7), ("panel", 0), ("sum1", 2), ("sum1", 6), ("sum2", 5),
+    ("sum0", 10), ("sum3", 3), ("launch", 11), ("sum1", 4), ("sum1", 8), ("sum0", 7), ("sum2", 2),
+    ("sum2", 6), ("sum3", 5), ("launch", 9), ("sum1", 10), ("sum0", 11), ("sum2", 4), ("sum2", 8),
+    ("sum1", 7), ("sum3", 2), ("panel", 2), ("sum3", 6), ("sum0", 9), ("sum2", 10), ("sum1", 11), ("sum3", 4),
+    ("panel", 4), ("sum3", 8), ("panel", 1), ("sum2", 7), ("sum1", 9), ("sum3", 10), ("panel", 3),
+    ("panel", 5), ("sum2", 11), ("sum3", 7), ("panel", 7), ("panel", 6), ("sum2", 9), ("panel", 8),
+    ("sum3", 11), ("panel", 10), ("sum3", 9), ("panel", 9), ("arrived", 0), ("diagonal", 0), ("diagonal", 1),
+    ("panel", 11), ("drain", 0), ("diagonal", 2), ("drain", 1), ("result", 0), ("result", 1), ("result", 2),
 )
 
 

time: 77.8 us -> 77 us (0.990)
  no operation moved by 1% of the time
where the time goes in v8:
time: 77 us; the launch traced here: 76.9 us
  Pallas kernels  75 us (97%)
  local copies, waits for them, and re-layouts  1.3 us (2%)
    pallas_call x1, Pallas kernels, body(): pl.pallas_call(kernel, out_shape=(pltpu.VMEM((ROWS * NSUP * 4, 128), F32)...  75 us

profile of v8, /device:TPU:7, one launch (start us, length us, event | category | flops | bytes accessed | tf_op | source)
XLA Modules:
  0.0 76.9 jit_solution(15198340926177756384)
XLA Ops:
  0.6 75.0 %level.1 = (f32[384,128]{1,0:T(8,128)S(1)}, f32[3,32,32]{2,1,0:T(8,128)S(1)}) custom-call(f32[512,512]{1,0:T(8,128)} %bitcast.5, f32[384,128]{1,0:T(8,128)} %bitcast.6, f32[3,32,32]{2,1,0:T(8,128)} %piv_hbm.1, s32[3,16]{1,0:T(4,128)} %bitcast.7), custom_call_target="tpu_custom_call" | custom-call | tf_op jit(solution)/shard_map/level/pallas_call | solution.py:471
  75.6 0.7 copy.10
  76.3 0.6 copy.11
